TPU v7x, 8 devices: a whole 2x2x1 slice. The times are simulated.
8 devices in a mesh: emb: 8 (over z, y, x, core).
Axes of the slice: x: 2, y: 2, z: 1, core: 2. Of those that a mesh axis runs over, the one named last changes fastest.
Arguments:
- uniq_ids: int32 [16384], P('emb')
- inv_map: int32 [32768], P('emb')
- x_in: bfloat16 [32768, 768], P('emb')
- d_out: bfloat16 [32768, 768], P('emb')
- tables: bfloat16 [5, 50304, 768], P(None, 'emb')
- w_up: bfloat16 [5, 768, 3072], replicated
- w_down: bfloat16 [5, 3072, 768], replicated
- w_gate: bfloat16 [5, 768, 768], replicated
- w_proj: bfloat16 [5, 768, 768], replicated
Outputs:
- output 1: bfloat16 [32768, 768], P('emb')
- output 2: float32 [5, 50304, 768], P(None, 'emb')
All inputs are finite; a program needn't handle non-finite values.
Results may differ from a plain program's by a relative error of at most 0.015214.
Values are sent between devices in bfloat16 or wider.
A program may use at most 1 GiB of HBM per device.

v0:
```python
import jax
import jax.numpy as jnp
from jax import lax
from jax.sharding import PartitionSpec as P

EPSILON = 1e-6


def gelu_tanh(pre_act):
    return jax.nn.gelu(pre_act, approximate=True)


def dot_nt(left, right):
    return lax.dot_general(left, right, (((1,), (1,)), ((), ())), preferred_element_type=jnp.float32)


def norm_rows(x):
    x_f = x.astype(jnp.float32)
    inv_rms = lax.rsqrt(jnp.mean(x_f * x_f, axis=-1, keepdims=True) + EPSILON)
    return x_f * inv_rms, inv_rms


def layer_forward(x, tok_rows, w_up, w_down, w_gate, w_proj):
    normed = norm_rows(x)[0]
    u_bf = normed.astype(jnp.bfloat16)
    hidden = gelu_tanh(jnp.dot(u_bf, w_up, preferred_element_type=jnp.float32)).astype(jnp.bfloat16)
    mlp_out = jnp.dot(hidden, w_down, preferred_element_type=jnp.float32).astype(jnp.bfloat16)
    gate_act = gelu_tanh(jnp.dot(u_bf, w_gate, preferred_element_type=jnp.float32)).astype(jnp.bfloat16)
    mixed = (gate_act.astype(jnp.float32) * tok_rows.astype(jnp.float32)).astype(jnp.bfloat16)
    proj_out = jnp.dot(mixed, w_proj, preferred_element_type=jnp.float32).astype(jnp.bfloat16)
    return (x.astype(jnp.float32) + mlp_out.astype(jnp.float32) + proj_out.astype(jnp.float32)).astype(jnp.bfloat16)


def layer_backward(x, tok_rows, cotangent, w_up, w_down, w_gate, w_proj, need_dx):
    normed, inv_rms = norm_rows(x)
    u_bf = normed.astype(jnp.bfloat16)
    pre_gate = jnp.dot(u_bf, w_gate, preferred_element_type=jnp.float32)
    gate_act = gelu_tanh(pre_gate).astype(jnp.bfloat16)
    d_mixed = dot_nt(cotangent, w_proj).astype(jnp.bfloat16)
    row_grad = gate_act.astype(jnp.float32) * d_mixed.astype(jnp.float32)
    if not need_dx:
        return cotangent, row_grad
    pre_up = jnp.dot(u_bf, w_up, preferred_element_type=jnp.float32)
    d_hidden = dot_nt(cotangent, w_down).astype(jnp.bfloat16)
    d_pre_up = jax.vjp(gelu_tanh, pre_up)[1](d_hidden.astype(jnp.float32))[0].astype(jnp.bfloat16)
    d_pre_gate = jax.vjp(gelu_tanh, pre_gate)[1](d_mixed.astype(jnp.float32) * tok_rows.astype(jnp.float32))[0].astype(jnp.bfloat16)
    d_normed = dot_nt(d_pre_up, w_up) + dot_nt(d_pre_gate, w_gate)
    d_x = inv_rms * (d_normed - normed * jnp.mean(d_normed * normed, axis=-1, keepdims=True))
    return (cotangent.astype(jnp.float32) + d_x).astype(jnp.bfloat16), row_grad


def solution(mesh):
    group_size = mesh.shape['emb']

    def body(uniq_loc, inv_loc, x_loc, dy_loc, tab_loc, w_up, w_down, w_gate, w_proj):
        layers = tab_loc.shape[0]
        shard_rows = tab_loc.shape[1]
        d_emb = tab_loc.shape[2]
        n_uniq = uniq_loc.shape[0]
        capacity = 2 * n_uniq // group_size
        my_dev = lax.axis_index('emb')
        owner_dev = uniq_loc // shard_rows
        owner_mask = (owner_dev[:, None] == jnp.arange(group_size)[None, :]).astype(jnp.int32)
        within_rank = jnp.sum((jnp.cumsum(owner_mask, axis=0) - owner_mask) * owner_mask, axis=1)
        dest_slot = owner_dev * capacity + within_rank
        send_ids = jnp.full((group_size * capacity,), -1, jnp.int32).at[dest_slot].set(uniq_loc)
        recv_ids = lax.all_to_all(send_ids.reshape(group_size, capacity), 'emb', 0, 0).reshape(-1)
        local_row = recv_ids - my_dev * shard_rows
        is_valid = recv_ids >= 0
        fetch_row = jnp.where(is_valid, local_row, 0)
        add_row = jnp.where(is_valid, local_row, shard_rows)
        tok_dest = jnp.take(dest_slot, inv_loc, axis=0)
        x = x_loc
        saved_x = []
        saved_rows = []
        for layer in range(layers):
            served = jnp.take(tab_loc[layer], fetch_row, axis=0)
            returned = lax.all_to_all(served.reshape(group_size, capacity, d_emb), 'emb', 0, 0)
            tok_rows = jnp.take(returned.reshape(group_size * capacity, d_emb), tok_dest, axis=0)
            saved_x.append(x)
            saved_rows.append(tok_rows)
            x = layer_forward(x, tok_rows, w_up[layer], w_down[layer], w_gate[layer], w_proj[layer])
        cotangent = dy_loc
        grad_list = [None] * layers
        for layer in reversed(range(layers)):
            cotangent, row_grad = layer_backward(saved_x[layer], saved_rows[layer], cotangent, w_up[layer],
                                                 w_down[layer], w_gate[layer], w_proj[layer], layer > 0)
            send_grad = jax.ops.segment_sum(row_grad, tok_dest, num_segments=group_size * capacity)
            recv_grad = lax.all_to_all(send_grad.reshape(group_size, capacity, d_emb), 'emb', 0, 0)
            grad_list[layer] = jax.ops.segment_sum(recv_grad.reshape(group_size * capacity, d_emb), add_row,
                                                   num_segments=shard_rows)
        return x, jnp.stack(grad_list)

    return jax.shard_map(body, mesh=mesh,
                         in_specs=(P('emb'), P('emb'), P('emb', None), P('emb', None), P(None, 'emb', None),
                                   P(), P(), P(), P()),
                         out_specs=(P('emb', None), P(None, 'emb', None)), check_vma=False)
```

profile of v0, /device:TPU:0, one launch (start us, length us, event | category | flops | bytes accessed | tf_op | source)
XLA Modules:
  0.0 2196.5 jit_solution(11552038294547630957)
XLA Ops:
  18.6 32.9 %slice_bitcast_fusion = (bf16[6288,768]{1,0:T(8,128)(2,1)}, bf16[6288,768]{1,0:T(8,128)(2,1)}, bf16[6288,768]{1,0:T(8,128)(2,1)}, bf16[6288,768]{1,0:T(8,128)(2,1)}, bf16[6288,768]{1,0:T(8,128)(2,1)}) fusion(bf16[5,6288,768]{2,1,0:T(8,128)(2,1)} %param.17), kind=kLoop, calls=%fused_computation.256 | loop fusion | bytes 96583680 | tf_op jit(solution)/shard_map/squeeze | solution.py:77
  242.0 38.4 %fusion.238.clone.5 = bf16[4096,3072]{1,0:T(8,128)(2,1)} fusion(bf16[4096,768]{0,1:T(8,128)(2,1)} %copy.16, f32[4096]{0:T(1024)S(1)} %add_rsqrt_fusion.4, bf16[5,768,3072]{2,1,0:T(8,128)(2,1)} %param.18), kind=kOutput, calls=%fused_computation.86.clone.clone.clone.clone.clone.clone.clone.clone.2 | convolution fusion | flops 19450036224 | bytes 36192256 | tf_op jit(solution)/shard_map/dot_general | solution.py:26
  460.2 36.0 %fusion.155 = (f32[4096]{0:T(1024)S(1)}, bf16[4096,768]{0,1:T(8,128)(2,1)}) fusion(bf16[4096,768]{0,1:T(8,128)(2,1)} %convolution_convert_fusion.8, bf16[5,3072,768]{2,1,0:T(8,128)(2,1)} %param.19, f32[4096,3072]{1,0:T(8,128)} %fusion.235, bf16[4096,768]{0,1:T(8,128)(2,1)} %get-tuple-element.27), kind=kOutput, calls=%fused_computation.232 | convolution fusion | flops 19472052224 | bytes 73940992 | tf_op jit(solution)/shard_map/dot_general | solution.py:27
  576.2 35.9 %fusion.158 = (f32[4096]{0:T(1024)S(1)}, bf16[4096,768]{0,1:T(8,128)(2,1)}) fusion(bf16[4096,768]{0,1:T(8,128)(2,1)} %convolution_convert_fusion.7, bf16[5,3072,768]{2,1,0:T(8,128)(2,1)} %param.19, f32[4096,3072]{1,0:T(8,128)} %fusion.231, bf16[4096,768]{0,1:T(8,128)(2,1)} %get-tuple-element.29), kind=kOutput, calls=%fused_computation.235 | convolution fusion | flops 19472052224 | bytes 73940992 | tf_op jit(solution)/shard_map/dot_general | solution.py:27
  692.2 36.0 %fusion.161 = (f32[4096]{0:T(1024)S(1)}, bf16[4096,768]{0,1:T(8,128)(2,1)}) fusion(bf16[4096,768]{0,1:T(8,128)(2,1)} %convolution_convert_fusion.6, bf16[5,3072,768]{2,1,0:T(8,128)(2,1)} %param.19, f32[4096,3072]{1,0:T(8,128)} %fusion.227, bf16[4096,768]{0,1:T(8,128)(2,1)} %get-tuple-element.31), kind=kOutput, calls=%fused_computation.238 | convolution fusion | flops 19472052224 | bytes 73940992 | tf_op jit(solution)/shard_map/dot_general | solution.py:27
  790.9 57.9 %fusion.177.clone.5 = bf16[4096,3072]{1,0:T(8,128)(2,1)} fusion(f32[4096,3072]{1,0:T(8,128)} %fusion.223, bf16[4096,768]{1,0:T(8,128)(2,1)} %param.16, bf16[5,3072,768]{2,1,0:T(8,128)(2,1)} %param.19), kind=kOutput, calls=%fused_computation.41.clone.clone.clone.clone.clone.clone.2 | convolution fusion | flops 19604176896 | bytes 86507520 | tf_op jit(solution)/shard_map/dot_general | solution.py:14
  912.0 59.0 %fusion.180.clone.5 = bf16[4096,3072]{1,0:T(8,128)(2,1)} fusion(f32[4096,3072]{1,0:T(8,128)} %fusion.227, bf16[4096,768]{0,1:T(8,128)(2,1)S(1)} %fusion.96, bf16[5,3072,768]{2,1,0:T(8,128)(2,1)} %param.19), kind=kOutput, calls=%fused_computation.46.clone.clone.clone.clone.clone.clone.2 | convolution fusion | flops 19604176896 | bytes 86507520 | tf_op jit(solution)/shard_map/dot_general | solution.py:14
  1038.0 59.0 %fusion.183.clone.5 = bf16[4096,3072]{1,0:T(8,128)(2,1)} fusion(f32[4096,3072]{1,0:T(8,128)} %fusion.231, bf16[4096,768]{0,1:T(8,128)(2,1)S(1)} %fusion.101, bf16[5,3072,768]{2,1,0:T(8,128)(2,1)} %param.19), kind=kOutput, calls=%fused_computation.51.clone.clone.clone.clone.clone.clone.2 | convolution fusion | flops 19604176896 | bytes 86507520 | tf_op jit(solution)/shard_map/dot_general | solution.py:14
  1163.4 60.4 %fusion.186.clone.5 = bf16[4096,3072]{1,0:T(8,128)(2,1)} fusion(f32[4096,3072]{1,0:T(8,128)} %fusion.235, bf16[4096,768]{0,1:T(8,128)(2,1)} %copy-done.3, bf16[5,3072,768]{2,1,0:T(8,128)(2,1)} %param.19), kind=kOutput, calls=%fused_computation.56.clone.clone.clone.clone.clone.clone.2 | convolution fusion | flops 19604176896 | bytes 86507520 | tf_op jit(solution)/shard_map/dot_general | solution.py:14
  1283.9 34.7 %scatter_custom_fusion.1 = f32[4096,768]{1,0:T(8,128)} fusion(s32[4096]{0:T(1024)} %copy-done.8, bf16[4096,768]{1,0:T(8,128)(2,1)} %fusion.151, bf16[4096,768]{1,0:T(8,128)(2,1)} %convolution_convert_fusion, f32[]{:T(128)} %constant.54.clone.1), kind=kCustom, calls=%fused_computation.160 | custom fusion | flops 12582912 | bytes 25166336 | tf_op jit(solution)/shard_map/scatter-add | solution.py:88
  1322.7 37.5 %scatter_custom_fusion.3 = f32[4096,768]{1,0:T(8,128)} fusion(s32[4096]{0:T(1024)} %copy-done.8, bf16[4096,768]{1,0:T(8,128)(2,1)} %copy-done.2, f32[]{:T(128)} %constant.54.clone.1, f32[4096,768]{1,0:T(8,128)} %fusion.233), kind=kCustom, calls=%fused_computation.168 | custom fusion | flops 40894464 | bytes 31457792 | tf_op jit(solution)/shard_map/scatter-add | solution.py:88
  1360.2 101.5 %all-to-all-done.6 = f32[8,512,768]{2,1,0:T(8,128)} async-done(((f32[8,512,768]{2,1,0:T(8,128)}), f32[8,512,768]{2,1,0:T(8,128)}, u32[]{:S(2)}, u32[]{:S(2)}) %all-to-all-start.6) | async-done | bytes 12582944 | tf_op jit(solution)/shard_map/all_to_all | solution.py:89
  1465.9 37.8 %scatter_custom_fusion.5 = f32[4096,768]{1,0:T(8,128)} fusion(s32[4096]{0:T(1024)} %copy-done.8, bf16[4096,768]{1,0:T(8,128)(2,1)} %convolution_convert_fusion.2, f32[]{:T(128)} %constant.54.clone.1, f32[4096,768]{1,0:T(8,128)} %fusion.229), kind=kCustom, calls=%fused_computation.167 | custom fusion | flops 40894464 | bytes 31457792 | tf_op jit(solution)/shard_map/scatter-add | solution.py:88
  1503.8 101.1 %all-to-all-done.7 = f32[8,512,768]{2,1,0:T(8,128)} async-done(((f32[8,512,768]{2,1,0:T(8,128)}), f32[8,512,768]{2,1,0:T(8,128)}, u32[]{:S(2)}, u32[]{:S(2)}) %all-to-all-start.7) | async-done | bytes 12582944 | tf_op jit(solution)/shard_map/all_to_all | solution.py:89
  1609.0 37.5 %scatter_custom_fusion.7 = f32[4096,768]{1,0:T(8,128)} fusion(s32[4096]{0:T(1024)} %copy-done.8, bf16[4096,768]{1,0:T(8,128)(2,1)} %convolution_convert_fusion.3, f32[]{:T(128)} %constant.54.clone.1, f32[4096,768]{1,0:T(8,128)} %fusion.225), kind=kCustom, calls=%fused_computation.166 | custom fusion | flops 40894464 | bytes 31457792 | tf_op jit(solution)/shard_map/scatter-add | solution.py:88
  1646.5 101.5 %all-to-all-done.8 = f32[8,512,768]{2,1,0:T(8,128)} async-done(((f32[8,512,768]{2,1,0:T(8,128)}), f32[8,512,768]{2,1,0:T(8,128)}, u32[]{:S(2)}, u32[]{:S(2)}) %all-to-all-start.8) | async-done | bytes 12582944 | tf_op jit(solution)/shard_map/all_to_all | solution.py:89
  1752.0 37.7 %scatter_custom_fusion.9 = f32[4096,768]{1,0:T(8,128)} fusion(s32[4096]{0:T(1024)} %copy-done.8, bf16[4096,768]{1,0:T(8,128)(2,1)} %convolution_convert_fusion.4, f32[]{:T(128)} %constant.54.clone.1, f32[4096,768]{1,0:T(8,128)} %fusion.221), kind=kCustom, calls=%fused_computation.165 | custom fusion | flops 40894464 | bytes 31457792 | tf_op jit(solution)/shard_map/scatter-add | solution.py:88
  1789.7 101.3 %all-to-all-done.9 = f32[8,512,768]{2,1,0:T(8,128)} async-done(((f32[8,512,768]{2,1,0:T(8,128)}), f32[8,512,768]{2,1,0:T(8,128)}, u32[]{:S(2)}, u32[]{:S(2)}) %all-to-all-start.9) | async-done | bytes 12582944 | tf_op jit(solution)/shard_map/all_to_all | solution.py:89
  1909.1 34.8 %fusion.163 = bf16[4096,768]{0,1:T(8,128)(2,1)} fusion(bf16[4096,768]{0,1:T(8,128)(2,1)} %get-tuple-element.33, bf16[4096,768]{0,1:T(8,128)(2,1)} %convolution_convert_fusion.5, f32[4096,3072]{1,0:T(8,128)} %fusion.223, bf16[5,3072,768]{2,1,0:T(8,128)(2,1)} %param.19), kind=kOutput, calls=%fused_computation.240 | convolution fusion | flops 19462619136 | bytes 73924608 | tf_op jit(solution)/shard_map/dot_general | solution.py:27
  1952.5 35.5 %scatter_custom_fusion.2 = f32[6288,768]{1,0:T(8,128)} fusion(s32[4096]{0:T(1024)} %bitcast.277, f32[4096,768]{1,0:T(8,128)} %bitcast.41, f32[]{:T(128)} %constant.54.clone.1), kind=kCustom, calls=%fused_computation.254 | custom fusion | flops 3145728 | bytes 19317248 | tf_op jit(solution)/shard_map/scatter-add | solution.py:90
  1988.0 35.3 %scatter_custom_fusion.4 = f32[6288,768]{1,0:T(8,128)} fusion(s32[4096]{0:T(1024)} %bitcast.278, f32[4096,768]{1,0:T(8,128)} %bitcast.44, f32[]{:T(128)} %constant.54.clone.1), kind=kCustom, calls=%fused_computation.252 | custom fusion | flops 3145728 | bytes 19317248 | tf_op jit(solution)/shard_map/scatter-add | solution.py:90
  2023.3 35.6 %scatter_custom_fusion.6 = f32[6288,768]{1,0:T(8,128)} fusion(s32[4096]{0:T(1024)} %bitcast.279, f32[4096,768]{1,0:T(8,128)} %bitcast.47, f32[]{:T(128)} %constant.54.clone.1), kind=kCustom, calls=%fused_computation.250 | custom fusion | flops 3145728 | bytes 19317248 | tf_op jit(solution)/shard_map/scatter-add | solution.py:90
  2058.9 35.2 %scatter_custom_fusion.8 = f32[6288,768]{1,0:T(8,128)} fusion(s32[4096]{0:T(1024)} %bitcast.280, f32[4096,768]{1,0:T(8,128)} %bitcast.50, f32[]{:T(128)} %constant.54.clone.1), kind=kCustom, calls=%fused_computation.248 | custom fusion | flops 3145728 | bytes 19317248 | tf_op jit(solution)/shard_map/scatter-add | solution.py:90
  2109.1 35.3 %scatter_custom_fusion.10 = f32[6288,768]{1,0:T(8,128)} fusion(s32[4096]{0:T(1024)} %bitcast.281, f32[4096,768]{1,0:T(8,128)} %bitcast.53, f32[]{:T(128)} %constant.54.clone.1), kind=kCustom, calls=%fused_computation.246 | custom fusion | flops 3145728 | bytes 19317248 | tf_op jit(solution)/shard_map/scatter-add | solution.py:90
  (173 shorter events, 977.2 us)
Async XLA Ops:
  14.3 79.3 %all-to-all-start = ((s32[8,1,512]{2,1,0:T(1,128)}), s32[8,1,512]{2,1,0:T(1,128)S(1)}, u32[]{:S(2)}, u32[]{:S(2)}) async-start(s32[8,1,512]{2,1,0:T(1,128)} %bitcast.5), calls=%async_computation | async-start | bytes 32768 | tf_op jit(solution)/shard_map/all_to_all | solution.py:67
  238.1 75.4 %all-to-all-start.1 = ((bf16[8,512,768]{2,1,0:T(8,128)(2,1)}), bf16[8,512,768]{2,1,0:T(8,128)(2,1)}, u32[]{:S(2)}, u32[]{:S(2)}) async-start(bf16[8,512,768]{2,1,0:T(8,128)(2,1)} %bitcast.268), calls=%async_computation.1 | async-start | bytes 12582912 | tf_op jit(solution)/shard_map/all_to_all | solution.py:78
  242.0 38.4 %copy-start = (s32[2048]{0:T(1024)S(1)}, s32[2048]{0:T(1024)}, u32[]{:S(2)}) copy-start(s32[2048]{0:T(1024)} %get-tuple-element.11) | copy-start | bytes 24580
  242.0 38.4 %copy-start.11 = (s32[4096]{0:T(1024)S(1)}, s32[4096]{0:T(1024)}, u32[]{:S(2)}) copy-start(s32[4096]{0:T(1024)} %get-tuple-element.42) | copy-start | bytes 49156
  303.5 375.1 %copy-start.14 = (pred[4096]{0:T(1024)(128)(4,1)}, pred[4096]{0:T(1024)(128)(4,1)S(1)}, u32[]{:S(2)}) copy-start(pred[4096]{0:T(1024)(128)(4,1)S(1)} %get-tuple-element.8) | copy-start | bytes 12292
  313.5 106.5 %all-to-all-start.2 = ((bf16[8,512,768]{2,1,0:T(8,128)(2,1)}), bf16[8,512,768]{2,1,0:T(8,128)(2,1)}, u32[]{:S(2)}, u32[]{:S(2)}) async-start(bf16[8,512,768]{2,1,0:T(8,128)(2,1)} %bitcast.267), calls=%async_computation.2 | async-start | bytes 12582912 | tf_op jit(solution)/shard_map/all_to_all | solution.py:78
  420.0 116.1 %all-to-all-start.3 = ((bf16[8,512,768]{2,1,0:T(8,128)(2,1)}), bf16[8,512,768]{2,1,0:T(8,128)(2,1)}, u32[]{:S(2)}, u32[]{:S(2)}) async-start(bf16[8,512,768]{2,1,0:T(8,128)(2,1)} %bitcast.266), calls=%async_computation.3 | async-start | bytes 12582912 | tf_op jit(solution)/shard_map/all_to_all | solution.py:78
  536.1 116.2 %all-to-all-start.4 = ((bf16[8,512,768]{2,1,0:T(8,128)(2,1)}), bf16[8,512,768]{2,1,0:T(8,128)(2,1)}, u32[]{:S(2)}, u32[]{:S(2)}) async-start(bf16[8,512,768]{2,1,0:T(8,128)(2,1)} %bitcast.265), calls=%async_computation.4 | async-start | bytes 12582912 | tf_op jit(solution)/shard_map/all_to_all | solution.py:78
  652.3 115.7 %all-to-all-start.5 = ((bf16[8,512,768]{2,1,0:T(8,128)(2,1)}), bf16[8,512,768]{2,1,0:T(8,128)(2,1)}, u32[]{:S(2)}, u32[]{:S(2)}) async-start(bf16[8,512,768]{2,1,0:T(8,128)(2,1)} %bitcast.264), calls=%async_computation.5 | async-start | bytes 12582912 | tf_op jit(solution)/shard_map/all_to_all | solution.py:78
  768.0 80.7 %slice-start.14 = ((s8[6291456]{0:T(1024)(128)(4,1)}), s8[2097152]{0:T(1024)(128)(4,1)S(1)}, s32[]{:S(2)}) async-start(s8[6291456]{0:T(1024)(128)(4,1)} %bitcast.271), calls=%async_computation.25 | async-start | bytes 4194304
  790.9 57.9 %slice-start.15 = ((s8[6291456]{0:T(1024)(128)(4,1)}), s8[4194304]{0:T(1024)(128)(4,1)S(1)}, s32[]{:S(2)}) async-start(s8[6291456]{0:T(1024)(128)(4,1)} %bitcast.271), calls=%async_computation.26 | async-start | bytes 8388608
  790.9 57.9 %copy-start.15 = (pred[4096]{0:T(1024)(128)(4,1)S(1)}, pred[4096]{0:T(1024)(128)(4,1)}, u32[]{:S(2)}) copy-start(pred[4096]{0:T(1024)(128)(4,1)} %copy-done.14) | copy-start | bytes 12292
  848.7 45.9 %slice-start.10 = ((s8[6291456]{0:T(1024)(128)(4,1)}), s8[4194304]{0:T(1024)(128)(4,1)S(1)}, s32[]{:S(2)}) async-start(s8[6291456]{0:T(1024)(128)(4,1)} %bitcast.262), calls=%async_computation.21 | async-start | bytes 8388608
  912.0 59.1 %copy-start.16 = (pred[4096]{0:T(1024)(128)(4,1)S(1)}, pred[4096]{0:T(1024)(128)(4,1)}, u32[]{:S(2)}) copy-start(pred[4096]{0:T(1024)(128)(4,1)} %copy-done.14) | copy-start | bytes 12292
  1038.0 59.0 %copy-start.17 = (pred[4096]{0:T(1024)(128)(4,1)S(1)}, pred[4096]{0:T(1024)(128)(4,1)}, u32[]{:S(2)}) copy-start(pred[4096]{0:T(1024)(128)(4,1)} %copy-done.14) | copy-start | bytes 12292
  1163.4 60.4 %copy-start.2 = (bf16[4096,768]{1,0:T(8,128)(2,1)}, bf16[4096,768]{1,0:T(8,128)(2,1)S(1)}, u32[]{:S(2)}) copy-start(bf16[4096,768]{1,0:T(8,128)(2,1)S(1)} %convolution_convert_fusion.1) | copy-start | bytes 18874372
  1163.4 60.4 %copy-start.18 = (pred[4096]{0:T(1024)(128)(4,1)S(1)}, pred[4096]{0:T(1024)(128)(4,1)}, u32[]{:S(2)}) copy-start(pred[4096]{0:T(1024)(128)(4,1)} %copy-done.14) | copy-start | bytes 12292
  1223.8 46.1 %slice-start.16 = ((s8[6291456]{0:T(1024)(128)(4,1)}), s8[2097152]{0:T(1024)(128)(4,1)S(1)}, s32[]{:S(2)}) async-start(s8[6291456]{0:T(1024)(128)(4,1)} %bitcast.273), calls=%async_computation.27 | async-start | bytes 4194304
  1318.6 143.1 %all-to-all-start.6 = ((f32[8,512,768]{2,1,0:T(8,128)}), f32[8,512,768]{2,1,0:T(8,128)}, u32[]{:S(2)}, u32[]{:S(2)}) async-start(f32[8,512,768]{2,1,0:T(8,128)} %bitcast.261), calls=%async_computation.6 | async-start | bytes 25165824 | tf_op jit(solution)/shard_map/all_to_all | solution.py:89
  1461.7 143.2 %all-to-all-start.7 = ((f32[8,512,768]{2,1,0:T(8,128)}), f32[8,512,768]{2,1,0:T(8,128)}, u32[]{:S(2)}, u32[]{:S(2)}) async-start(f32[8,512,768]{2,1,0:T(8,128)} %bitcast.258), calls=%async_computation.7 | async-start | bytes 25165824 | tf_op jit(solution)/shard_map/all_to_all | solution.py:89
  1604.9 143.0 %all-to-all-start.8 = ((f32[8,512,768]{2,1,0:T(8,128)}), f32[8,512,768]{2,1,0:T(8,128)}, u32[]{:S(2)}, u32[]{:S(2)}) async-start(f32[8,512,768]{2,1,0:T(8,128)} %bitcast.259), calls=%async_computation.8 | async-start | bytes 25165824 | tf_op jit(solution)/shard_map/all_to_all | solution.py:89
  1747.9 143.0 %all-to-all-start.9 = ((f32[8,512,768]{2,1,0:T(8,128)}), f32[8,512,768]{2,1,0:T(8,128)}, u32[]{:S(2)}, u32[]{:S(2)}) async-start(f32[8,512,768]{2,1,0:T(8,128)} %bitcast.260), calls=%async_computation.9 | async-start | bytes 25165824 | tf_op jit(solution)/shard_map/all_to_all | solution.py:89
  1891.0 218.1 %all-to-all-start.10 = ((f32[8,512,768]{2,1,0:T(8,128)}), f32[8,512,768]{2,1,0:T(8,128)}, u32[]{:S(2)}, u32[]{:S(2)}) async-start(f32[8,512,768]{2,1,0:T(8,128)} %bitcast.257), calls=%async_computation.10 | async-start | bytes 25165824 | tf_op jit(solution)/shard_map/all_to_all | solution.py:89
  2144.4 33.6 %slice-start.2 = ((s8[19316736]{0:T(1024)(128)(4,1)}), s8[4194304]{0:T(1024)(128)(4,1)S(1)}, s32[]{:S(2)}) async-start(s8[19316736]{0:T(1024)(128)(4,1)} %bitcast.253), calls=%async_computation.13 | async-start | bytes 8388608
  (24 other events, 421.1 us)
where the time goes:
time: 2210 us; the launch traced here: 2200 us
  matrix products  920 us (42%)
  other arithmetic  421 us (19%)
  waiting for transfers between devices  415 us (19%)
  local copies, waits for them, and re-layouts  395 us (18%)
  starting transfers between devices  44.2 us (2%)
    dot_general x17, matrix products, dot_nt(): lax.dot_general(left, right, (((1,), (1,)), ((), ())), preferred_element_...  473 us
    all_to_all x5, waiting for transfers between devices, body(): lax.all_to_all(send_grad.reshape(group_size, capacity, d_emb), 'emb', 0, 0)  405 us
    scatter-add x5, other arithmetic, body(): jax.ops.segment_sum(row_grad, tok_dest, num_segments=group_size * capacity)  185 us
    scatter-add x5, other arithmetic, body(): jax.ops.segment_sum(recv_grad.reshape(group_size * capacity, d_emb), add_...  177 us
    dot_general x5, matrix products, layer_forward(): jnp.dot(hidden, w_down, preferred_element_type=jnp.float32)  172 us
    dot_general x5, matrix products, layer_forward(): jnp.dot(u_bf, w_up, preferred_element_type=jnp.float32)  157 us
    gather x5, local copies, waits for them, and re-layouts, body(): served = jnp.take(tab_loc[layer], fetch_row, axis=0)  120 us
    gather x5, local copies, waits for them, and re-layouts, body(): jnp.take(returned.reshape(group_size * capacity, d_emb), tok_dest, axis=0)  114 us
  transfers between devices with their start and end apart: 11, of which 5 were waited for; matrix products, arithmetic and copies ran while one was open for 43% of the time, Pallas kernels for 0%

commit v1 on v0

v1 whole, which is shorter than its diff:
```python
import functools

import jax
import jax.numpy as jnp
from jax import lax
from jax.experimental import pallas as pl
from jax.experimental.pallas import tpu as pltpu
from jax.sharding import PartitionSpec as P

EPSILON = 1e-6
BF16 = jnp.bfloat16
F32 = jnp.float32
I32 = jnp.int32

CH = 16
SUB = 256
WIN = 384
TB = 512
FC = 512
VMEM_LIMIT = 60 * 1024 * 1024
G0 = 0.7978845608028654
G1 = G0 * 0.044715


def dot(a, b):
    return jnp.dot(a, b, preferred_element_type=F32)


def dot_nt(a, b):
    return lax.dot_general(a, b, (((1,), (1,)), ((), ())), preferred_element_type=F32)


def gelu(a):
    half = 0.5 * a
    return half * jnp.tanh(a * (G0 + G1 * (a * a))) + half


def gelu_grad(a):
    sq = a * a
    t = jnp.tanh(a * (G0 + G1 * sq))
    return 0.5 * t + 0.5 + (0.5 * a * (1.0 - t * t)) * (G0 + (3.0 * G1) * sq)


def norm_rows(xf):
    inv = lax.rsqrt(jnp.mean(xf * xf, axis=-1, keepdims=True) + EPSILON)
    return xf * inv, inv


def fwd_kernel(wst, chunk, x_ref, posc_ref, up_ref, dn_ref, gt_ref, pj_ref, ret_ref,
               xo_ref, e_ref, rows, sem):
    i = pl.program_id(0)
    n_rows = rows.shape[0]

    @pl.when(i == 0)
    def _():
        def start(d, carry):
            src = pl.multiple_of(chunk[d] * CH, CH)
            dst = pl.multiple_of(d * CH, CH)
            pltpu.make_async_copy(ret_ref.at[pl.ds(src, CH)], rows.at[pl.ds(dst, CH)], sem).start()
            return carry

        lax.fori_loop(0, n_rows // CH, start, 0)
        pltpu.make_async_copy(ret_ref.at[pl.ds(0, n_rows)], rows, sem).wait()

    tb = x_ref.shape[0]
    xf = x_ref[...].astype(F32)
    u = norm_rows(xf)[0].astype(BF16)
    parts = []
    for q in range(tb // SUB):
        w0 = pl.multiple_of(wst[i * (tb // SUB) + q] * CH, CH)
        col = posc_ref[q * SUB:(q + 1) * SUB, :] - w0
        hot = jnp.where(col == lax.broadcasted_iota(I32, (SUB, WIN), 1), 1.0, 0.0).astype(BF16)
        parts.append(dot(hot, rows[pl.ds(w0, WIN), :]).astype(BF16))
    e = jnp.concatenate(parts, axis=0)
    e_ref[...] = e
    g = gelu(dot(u, gt_ref[0])).astype(BF16)
    z = (g.astype(F32) * e.astype(F32)).astype(BF16)
    proj = dot(z, pj_ref[0]).astype(BF16)
    ff = up_ref.shape[2]
    mlp = None
    for k in range(ff // FC):
        h = gelu(dot(u, up_ref[0, :, k * FC:(k + 1) * FC])).astype(BF16)
        part = dot(h, dn_ref[0, k * FC:(k + 1) * FC, :])
        mlp = part if mlp is None else mlp + part
    xo_ref[...] = (xf + mlp.astype(BF16).astype(F32) + proj.astype(F32)).astype(BF16)


def rowgrad_kernel(wst, chunk, total, x_ref, c_ref, posr_ref, gt_ref, pj_ref,
                   s_ref, send_ref, acc, sem):
    i = pl.program_id(0)
    last = pl.num_programs(0) - 1

    @pl.when(i == 0)
    def _():
        acc[...] = jnp.zeros_like(acc)

    tb = x_ref.shape[0]
    u = norm_rows(x_ref[...].astype(F32))[0].astype(BF16)
    g = gelu(dot(u, gt_ref[0])).astype(BF16)
    s = dot_nt(c_ref[...], pj_ref[0]).astype(BF16)
    s_ref[...] = s
    k = g.astype(F32) * s.astype(F32)
    hi = k.astype(BF16)
    lo = (k - hi.astype(F32)).astype(BF16)
    for q in range(tb // SUB):
        w0 = pl.multiple_of(wst[i * (tb // SUB) + q] * CH, CH)
        row = posr_ref[q] - w0
        hot = jnp.where(row == lax.broadcasted_iota(I32, (WIN, SUB), 0), 1.0, 0.0).astype(BF16)
        sl = slice(q * SUB, (q + 1) * SUB)
        acc[pl.ds(w0, WIN), :] += dot(hot, hi[sl]) + dot(hot, lo[sl])

    @pl.when(i == last)
    def _():
        def copy(d):
            dst = pl.multiple_of(chunk[d] * CH, CH)
            src = pl.multiple_of(d * CH, CH)
            return pltpu.make_async_copy(acc.at[pl.ds(src, CH)], send_ref.at[pl.ds(dst, CH)], sem)

        def start(d, carry):
            copy(d).start()
            return carry

        def wait(d, carry):
            copy(d).wait()
            return carry

        lax.fori_loop(0, total[0], start, 0)
        lax.fori_loop(0, total[0], wait, 0)


def bwd_kernel(x_ref, c_ref, s_ref, e_ref, up_ref, dn_ref, gt_ref, co_ref):
    xf = x_ref[...].astype(F32)
    n, inv = norm_rows(xf)
    u = n.astype(BF16)
    c = c_ref[...]
    b = dot(u, gt_ref[0])
    db = (gelu_grad(b) * (s_ref[...].astype(F32) * e_ref[...].astype(F32))).astype(BF16)
    du = dot_nt(db, gt_ref[0])
    ff = up_ref.shape[2]
    for k in range(ff // FC):
        w_k = up_ref[0, :, k * FC:(k + 1) * FC]
        a = dot(u, w_k)
        dh = dot_nt(c, dn_ref[0, k * FC:(k + 1) * FC, :]).astype(BF16)
        da = (gelu_grad(a) * dh.astype(F32)).astype(BF16)
        du = du + dot_nt(da, w_k)
    dx = inv * (du - n * jnp.mean(du * n, axis=-1, keepdims=True))
    co_ref[...] = (c.astype(F32) + dx).astype(BF16)


def scatter_body(layer, row_of, count, recv_ref, out_ref, acc, sem):
    i = pl.program_id(0)
    cap = recv_ref.shape[0]

    @pl.when(i == 0)
    def _():
        acc[...] = jnp.zeros_like(acc)

    def group(t, carry):
        base = pl.multiple_of(t * 8, 8)
        idx = [row_of[i * cap + base + q] for q in range(8)]
        old = [acc[pl.ds(r, 1), :] for r in idx]
        new = [o + recv_ref[pl.ds(base + q, 1), :] for q, o in enumerate(old)]
        for r, v in zip(idx, new):
            acc[pl.ds(r, 1), :] = v
        return carry

    lax.fori_loop(0, (count[i] + 7) // 8, group, 0)

    @pl.when(i == pl.num_programs(0) - 1)
    def _():
        cp = pltpu.make_async_copy(acc.at[pl.ds(0, out_ref.shape[1])], out_ref.at[layer], sem)
        cp.start()
        cp.wait()


def scatter_first(layer, row_of, count, recv_ref, out_ref, acc, sem):
    scatter_body(layer, row_of, count, recv_ref, out_ref, acc, sem)


def scatter_next(layer, row_of, count, recv_ref, _, out_ref, acc, sem):
    scatter_body(layer, row_of, count, recv_ref, out_ref, acc, sem)


ANY = pl.BlockSpec(memory_space=pl.ANY)


def once(shape, index_map):
    return pl.BlockSpec(shape, index_map, pipeline_mode=pl.Buffered(1))


def params():
    return pltpu.CompilerParams(dimension_semantics=("arbitrary",), vmem_limit_bytes=VMEM_LIMIT)


def cost(flops, nbytes):
    return pl.CostEstimate(flops=int(flops), bytes_accessed=int(nbytes), transcendentals=0)


def solution(mesh):
    group_size = mesh.shape['emb']

    def body(uniq_loc, inv_loc, x_loc, dy_loc, tab_loc, w_up, w_down, w_gate, w_proj):
        layers, shard_rows, d_emb = tab_loc.shape
        n_uniq = uniq_loc.shape[0]
        n_tok, d_model = x_loc.shape
        ff = w_up.shape[2]
        capacity = 2 * n_uniq // group_size
        slots = group_size * capacity
        cap_ch = capacity // CH
        row_chunks = (n_uniq + group_size * CH + WIN) // CH
        n_rows = row_chunks * CH
        my_dev = lax.axis_index('emb')

        iota = jnp.arange(n_tok, dtype=I32)
        tok_id = uniq_loc.at[inv_loc].get(mode='promise_in_bounds')
        order = lax.sort(tok_id * n_tok + iota)
        perm = order % n_tok
        sid = order // n_tok
        unperm = lax.sort(perm * n_tok + iota) % n_tok
        is_new = jnp.concatenate([jnp.ones((1,), jnp.bool_), sid[1:] != sid[:-1]])
        rank = jnp.cumsum(is_new.astype(I32)) - 1
        used = lax.sort(jnp.where(is_new, sid, jnp.int32(2 ** 30)))[:n_uniq]
        owners = jnp.arange(group_size, dtype=I32)
        own = sid // shard_rows
        own_hot = own[None, :] == owners[:, None]
        cnt = jnp.sum(jnp.where(own_hot & is_new[None, :], 1, 0), axis=1).astype(I32)
        first = (jnp.cumsum(cnt) - cnt).astype(I32)
        n_ch = (cnt + CH - 1) // CH
        first_ch = (jnp.cumsum(n_ch) - n_ch).astype(I32)
        pos = rank + jnp.sum(jnp.where(own_hot, (first_ch * CH - first)[:, None], 0), axis=0)
        pos = pos.astype(I32)
        wst = pos.reshape(n_tok // SUB, SUB)[:, 0] // CH
        cid = jnp.arange(row_chunks, dtype=I32)[None, :]
        in_own = (cid >= first_ch[:, None]) & (cid < (first_ch + n_ch)[:, None])
        chunk = jnp.sum(jnp.where(in_own, owners[:, None] * cap_ch + cid - first_ch[:, None], 0), axis=0).astype(I32)
        total = jnp.sum(n_ch).astype(I32).reshape(1)
        used_pad = jnp.concatenate([used, jnp.full((capacity,), -1, I32)])
        kk = jnp.arange(capacity, dtype=I32)
        send_ids = jnp.stack([
            jnp.where(kk < cnt[j], lax.dynamic_slice(used_pad, (first[j],), (capacity,)), -1)
            for j in range(group_size)])
        recv_ids = lax.all_to_all(send_ids, 'emb', 0, 0)
        valid = recv_ids >= 0
        local_row = recv_ids - my_dev * shard_rows
        fetch_row = jnp.where(valid, local_row, 0).reshape(-1)
        add_row = jnp.where(valid, local_row, shard_rows).reshape(-1)
        add_cnt = jnp.sum(valid.astype(I32), axis=1).astype(I32)
        posc = pos.reshape(n_tok, 1)
        posr = pos.reshape(n_tok // SUB, 1, SUB)
        flat_tab = tab_loc.reshape(layers * shard_rows, d_emb)

        tok_spec = pl.BlockSpec((TB, d_model), lambda i, *_: (i, 0))
        posr_spec = pl.BlockSpec((TB // SUB, 1, SUB), lambda i, *_: (i, 0, 0))
        grid = (n_tok // TB,)
        tok_out = jax.ShapeDtypeStruct((n_tok, d_model), BF16)

        def w_specs(layer, *shapes):
            return [once((1,) + s, lambda i, *_, layer=layer: (layer, 0, 0)) for s in shapes]

        s_up, s_dn, s_sq = (d_model, ff), (ff, d_model), (d_model, d_emb)
        mm = 2.0 * n_tok * d_model * ff
        sq = 2.0 * n_tok * d_model * d_emb

        def forward(layer, x, returned):
            return pl.pallas_call(
                fwd_kernel, out_shape=[tok_out, tok_out],
                grid_spec=pltpu.PrefetchScalarGridSpec(
                    num_scalar_prefetch=2, grid=grid,
                    in_specs=[tok_spec, pl.BlockSpec((TB, 1), lambda i, *_: (i, 0)),
                              *w_specs(layer, s_up, s_dn, s_sq, s_sq), ANY],
                    out_specs=[tok_spec, tok_spec],
                    scratch_shapes=[pltpu.VMEM((n_rows, d_emb), BF16), pltpu.SemaphoreType.DMA]),
                compiler_params=params(), name='fwd',
                cost_estimate=cost(2 * mm + 2 * sq, 3e7),
            )(wst, chunk, x, posc, w_up, w_down, w_gate, w_proj, returned)

        def rowgrad(layer, x, c):
            return pl.pallas_call(
                rowgrad_kernel, out_shape=[tok_out, jax.ShapeDtypeStruct((slots, d_emb), F32)],
                grid_spec=pltpu.PrefetchScalarGridSpec(
                    num_scalar_prefetch=3, grid=grid,
                    in_specs=[tok_spec, tok_spec, posr_spec, *w_specs(layer, s_sq, s_sq)],
                    out_specs=[tok_spec, ANY],
                    scratch_shapes=[pltpu.VMEM((n_rows, d_emb), F32), pltpu.SemaphoreType.DMA]),
                compiler_params=params(), name='rowgrad',
                cost_estimate=cost(2 * sq, 3e7),
            )(wst, chunk, total, x, c, posr, w_gate, w_proj)

        def backward(layer, x, c, s, e):
            return pl.pallas_call(
                bwd_kernel, out_shape=tok_out, grid=grid,
                in_specs=[tok_spec] * 4 + w_specs(layer, s_up, s_dn, s_sq),
                out_specs=tok_spec,
                compiler_params=params(), name='bwd',
                cost_estimate=cost(3 * mm + 2 * sq, 4e7),
            )(x, c, s, e, w_up, w_down, w_gate)

        def scatter(layer, received, grads):
            ins = [pl.BlockSpec((capacity, d_emb), lambda i, *_: (i, 0))]
            args = [received]
            if grads is not None:
                ins.append(ANY)
                args.append(grads)
            return pl.pallas_call(
                functools.partial(scatter_first if grads is None else scatter_next, layer),
                out_shape=jax.ShapeDtypeStruct((layers, shard_rows, d_emb), F32),
                grid_spec=pltpu.PrefetchScalarGridSpec(
                    num_scalar_prefetch=2, grid=(group_size,), in_specs=ins, out_specs=ANY,
                    scratch_shapes=[pltpu.VMEM((shard_rows + 8, d_emb), F32), pltpu.SemaphoreType.DMA]),
                compiler_params=params(), name='scatter',
                input_output_aliases={} if grads is None else {3: 0},
                cost_estimate=cost(1e10, 4e7),
            )(add_row, add_cnt, *args)

        def serve(layer, index):
            rows = flat_tab.at[index + layer * shard_rows].get(mode='promise_in_bounds')
            return rows.reshape(group_size, capacity, d_emb)

        def exchange(a):
            return lax.all_to_all(a, 'emb', 0, 0)

        served = serve(0, fetch_row)
        got = exchange(served)
        perm, served, later = lax.optimization_barrier((perm, served, fetch_row))
        x = x_loc.at[perm].get(mode='promise_in_bounds')
        c = dy_loc.at[perm].get(mode='promise_in_bounds')
        served = serve(1, later)
        saved_x, saved_e = [], []
        for layer in range(layers):
            here = got
            if layer + 1 < layers:
                x, c, here, served, later = lax.optimization_barrier((x, c, here, served, later))
                got = exchange(served)
                if layer + 2 < layers:
                    served = serve(layer + 2, later)
            saved_x.append(x)
            x, e = forward(layer, x, here.reshape(slots, d_emb))
            saved_e.append(e)
        x_out = x.at[unperm].get(mode='promise_in_bounds')

        grads = None
        pending = None
        for layer in reversed(range(layers)):
            s, send = rowgrad(layer, saved_x[layer], c)
            got = lax.all_to_all(send.reshape(group_size, capacity, d_emb), 'emb', 0, 0).reshape(slots, d_emb)
            if pending is not None:
                c, pending = lax.optimization_barrier((c, pending))
                grads = scatter(layer + 1, pending, grads)
            if layer > 0:
                c = backward(layer, saved_x[layer], c, s, saved_e[layer])
            pending = got
        grads = scatter(0, pending, grads)
        return x_out, grads

    return jax.shard_map(body, mesh=mesh,
                         in_specs=(P('emb'), P('emb'), P('emb', None), P('emb', None), P(None, 'emb', None),
                                   P(), P(), P(), P()),
                         out_specs=(P('emb', None), P(None, 'emb', None)), check_vma=False)
```

time: 2210 us -> 2100 us (0.950)
  Pallas kernels: 0 us -> 1020 us
  matrix products: 920 us -> 0 us
  starting transfers between devices: 44.2 us -> 480 us
  other arithmetic: 421 us -> 32.5 us
  waiting for transfers between devices: 415 us -> 68.6 us
  local copies, waits for them, and re-layouts: 395 us -> 470 us
    pallas_call x0 -> x19, Pallas kernels: none -> 1020 us  [the longest x4 361 us: backward(): pl.pallas_call(bwd_kernel, out_shape=tok_out, grid=grid, in_specs=[tok_sp...]
    dot_general x37 -> x0, matrix products: 920 us -> none  [the longest x17 473 us: dot_nt(): lax.dot_general(left, right, (((1,), (1,)), ((), ())), preferred_element_...]
    all_to_all x11, starting transfers between devices: 44.2 us -> 480 us  [the longest x5 453 us: exchange(): return lax.all_to_all(a, 'emb', 0, 0)]
    scatter-add x10 -> x0, other arithmetic: 362 us -> none  [the longest x5 185 us: body(): jax.ops.segment_sum(row_grad, tok_dest, num_segments=group_size * capacity)]
    all_to_all x11, waiting for transfers between devices: 415 us -> 68.6 us  [the longest x5 64 us: body(): lax.all_to_all(send.reshape(group_size, capacity, d_emb), 'emb', 0, 0)]
    gather x11 -> x9, local copies, waits for them, and re-layouts: 257 us -> 465 us  [the longest x5 374 us: serve(): rows = flat_tab.at[index + layer * shard_rows].get(mode='promise_in_bounds')]
    unnamed x81 -> x21, local copies, waits for them, and re-layouts: 89.1 us -> 0.06 us
    squeeze x1 -> x0, local copies, waits for them, and re-layouts: 32.9 us -> none  [body(): served = jnp.take(tab_loc[layer], fetch_row, axis=0)]
  transfers between devices with their start and end apart: 11 -> 11, of which waited for: 5 -> 4; matrix products, arithmetic and copies ran while one was open for 43% -> 18% of each run, Pallas kernels for 0% -> 47%
where the time goes in v1:
time: 2100 us; the launch traced here: 2090 us
  Pallas kernels  1020 us (49%)
  starting transfers between devices  480 us (23%)
  local copies, waits for them, and re-layouts  470 us (22%)
  waiting for transfers between devices  68.6 us (3%)
  other arithmetic  32.5 us (2%)
    all_to_all x5, starting transfers between devices, exchange(): return lax.all_to_all(a, 'emb', 0, 0)  453 us
    gather x5, local copies, waits for them, and re-layouts, serve(): rows = flat_tab.at[index + layer * shard_rows].get(mode='promise_in_bounds')  374 us
    pallas_call x4, Pallas kernels, backward(): pl.pallas_call(bwd_kernel, out_shape=tok_out, grid=grid, in_specs=[tok_sp...  361 us
    pallas_call x5, Pallas kernels, forward(): pl.pallas_call(fwd_kernel, out_shape=[tok_out, tok_out], grid_spec=pltpu....  353 us
    pallas_call x5, Pallas kernels, scatter(): pl.pallas_call(functools.partial(scatter_first if grads is None else scat...  170 us
    pallas_call x5, Pallas kernels, rowgrad(): pl.pallas_call(rowgrad_kernel, out_shape=[tok_out, jax.ShapeDtypeStruct((...  136 us
    all_to_all x5, waiting for transfers between devices, body(): lax.all_to_all(send.reshape(group_size, capacity, d_emb), 'emb', 0, 0)  64 us
  transfers between devices with their start and end apart: 11, of which 4 were waited for; matrix products, arithmetic and copies ran while one was open for 18% of the time, Pallas kernels for 47%

profile of v1, /device:TPU:0, one launch (start us, length us, event | category | flops | bytes accessed | tf_op | source)
XLA Modules:
  0.0 2088.9 jit_solution(16914392113922333617)
XLA Ops:
  70.6 74.9 %gather_fusion.1 = bf16[4096,768]{1,0:T(8,128)(2,1)} fusion(bf16[31440,768]{1,0:T(8,128)(2,1)} %bitcast.69, s32[4096]{0:T(1024)S(1)} %broadcast_clamp_fusion), kind=kCustom, calls=%fused_computation.1 | custom fusion | bytes 12599296 | tf_op jit(solution)/shard_map/gather | solution.py:316
  145.4 86.9 %all-to-all-start.1 = ((bf16[8,512,768]{2,1,0:T(8,128)(2,1)}), bf16[8,512,768]{2,1,0:T(8,128)(2,1)}, u32[]{:S(2)}, u32[]{:S(2)}) async-start(bf16[8,512,768]{2,1,0:T(8,128)(2,1)} %bitcast.75), calls=%async_computation.1 | async-start | bytes 12582912 | tf_op jit(solution)/shard_map/all_to_all | solution.py:320
  233.2 74.8 %gather_fusion.4 = bf16[4096,768]{1,0:T(8,128)(2,1)} fusion(bf16[31440,768]{1,0:T(8,128)(2,1)} %bitcast.70, s32[4096]{0:T(1024)S(1)} %fusion.4), kind=kCustom, calls=%fused_computation.4 | custom fusion | bytes 12599296 | tf_op jit(solution)/shard_map/gather | solution.py:316
  353.4 90.5 %all-to-all-start.2 = ((bf16[8,512,768]{2,1,0:T(8,128)(2,1)}), bf16[8,512,768]{2,1,0:T(8,128)(2,1)}, u32[]{:S(2)}, u32[]{:S(2)}) async-start(bf16[8,512,768]{2,1,0:T(8,128)(2,1)} %bitcast.74), calls=%async_computation.2 | async-start | bytes 12582912 | tf_op jit(solution)/shard_map/all_to_all | solution.py:320
  451.4 74.8 %gather_fusion.5 = bf16[4096,768]{1,0:T(8,128)(2,1)} fusion(bf16[31440,768]{1,0:T(8,128)(2,1)} %bitcast.71, s32[4096]{0:T(1024)S(1)} %fusion.5), kind=kCustom, calls=%fused_computation.5 | custom fusion | bytes 12599296 | tf_op jit(solution)/shard_map/gather | solution.py:316
  526.2 70.6 %fwd.5 = (bf16[4096,768]{1,0:T(8,128)(2,1)}, bf16[4096,768]{1,0:T(8,128)(2,1)}) custom-call(s32[16]{0:T(128)} %and_select_fusion.wst, s32[160]{0:T(256)} %select_reduce_fusion.2.chunk, bf16[4096,768]{1,0:T(8,128)(2,1)} %gather_fusion.2, s32[4096,1]{1,0:T(8,128)} %add.223.posc_ref, bf16[5,768,3072]{2,1,0:T(8,128)(2,1)} %up_ref.17, ...), custom_call_target="tpu_custom_call" | custom-call | flops 48318382080 | bytes 30000000 | tf_op jit(solution)/shard_map/fwd/pallas_call | solution.py:265
  596.8 92.1 %all-to-all-start.3 = ((bf16[8,512,768]{2,1,0:T(8,128)(2,1)}), bf16[8,512,768]{2,1,0:T(8,128)(2,1)}, u32[]{:S(2)}, u32[]{:S(2)}) async-start(bf16[8,512,768]{2,1,0:T(8,128)(2,1)} %bitcast.77), calls=%async_computation.3 | async-start | bytes 12582912 | tf_op jit(solution)/shard_map/all_to_all | solution.py:320
  688.9 74.9 %gather_fusion.6 = bf16[4096,768]{1,0:T(8,128)(2,1)} fusion(bf16[31440,768]{1,0:T(8,128)(2,1)} %bitcast.72, s32[4096]{0:T(1024)S(1)} %fusion.6), kind=kCustom, calls=%fused_computation.6 | custom fusion | bytes 12599296 | tf_op jit(solution)/shard_map/gather | solution.py:316
  763.8 70.7 %fwd.6 = (bf16[4096,768]{1,0:T(8,128)(2,1)}, bf16[4096,768]{1,0:T(8,128)(2,1)}) custom-call(s32[16]{0:T(128)} %and_select_fusion.wst, s32[160]{0:T(256)} %select_reduce_fusion.2.chunk, bf16[4096,768]{1,0:T(8,128)(2,1)} %get-tuple-element.64.x_ref, s32[4096,1]{1,0:T(8,128)} %add.223.posc_ref, bf16[5,768,3072]{2,1,0:T(8,128)(2,1)} %up_ref.17, ...), custom_call_target="tpu_custom_call" | custom-call | flops 48318382080 | bytes 30000000 | tf_op jit(solution)/shard_map/fwd/pallas_call | solution.py:265
  834.4 92.0 %all-to-all-start.4 = ((bf16[8,512,768]{2,1,0:T(8,128)(2,1)}), bf16[8,512,768]{2,1,0:T(8,128)(2,1)}, u32[]{:S(2)}, u32[]{:S(2)}) async-start(bf16[8,512,768]{2,1,0:T(8,128)(2,1)} %bitcast.78), calls=%async_computation.4 | async-start | bytes 12582912 | tf_op jit(solution)/shard_map/all_to_all | solution.py:320
  926.5 74.9 %gather_fusion.7 = bf16[4096,768]{1,0:T(8,128)(2,1)} fusion(bf16[31440,768]{1,0:T(8,128)(2,1)} %bitcast.73, s32[4096]{0:T(1024)S(1)} %fusion.7), kind=kCustom, calls=%fused_computation.7 | custom fusion | bytes 12599296 | tf_op jit(solution)/shard_map/gather | solution.py:316
  1001.4 70.7 %fwd.7 = (bf16[4096,768]{1,0:T(8,128)(2,1)}, bf16[4096,768]{1,0:T(8,128)(2,1)}) custom-call(s32[16]{0:T(128)} %and_select_fusion.wst, s32[160]{0:T(256)} %select_reduce_fusion.2.chunk, bf16[4096,768]{1,0:T(8,128)(2,1)} %get-tuple-element.70.x_ref, s32[4096,1]{1,0:T(8,128)} %add.223.posc_ref, bf16[5,768,3072]{2,1,0:T(8,128)(2,1)} %up_ref.17, ...), custom_call_target="tpu_custom_call" | custom-call | flops 48318382080 | bytes 30000000 | tf_op jit(solution)/shard_map/fwd/pallas_call | solution.py:265
  1072.1 91.8 %all-to-all-start.5 = ((bf16[8,512,768]{2,1,0:T(8,128)(2,1)}), bf16[8,512,768]{2,1,0:T(8,128)(2,1)}, u32[]{:S(2)}, u32[]{:S(2)}) async-start(bf16[8,512,768]{2,1,0:T(8,128)(2,1)} %bitcast.76), calls=%async_computation.5 | async-start | bytes 12582912 | tf_op jit(solution)/shard_map/all_to_all | solution.py:320
  1164.5 70.6 %fwd.8 = (bf16[4096,768]{1,0:T(8,128)(2,1)}, bf16[4096,768]{1,0:T(8,128)(2,1)}) custom-call(s32[16]{0:T(128)} %and_select_fusion.wst, s32[160]{0:T(256)} %select_reduce_fusion.2.chunk, bf16[4096,768]{1,0:T(8,128)(2,1)} %get-tuple-element.76.x_ref, s32[4096,1]{1,0:T(8,128)} %add.223.posc_ref, bf16[5,768,3072]{2,1,0:T(8,128)(2,1)} %up_ref.17, ...), custom_call_target="tpu_custom_call" | custom-call | flops 48318382080 | bytes 30000000 | tf_op jit(solution)/shard_map/fwd/pallas_call | solution.py:265
  1267.0 70.7 %fwd.9 = (bf16[4096,768]{1,0:T(8,128)(2,1)}, bf16[4096,768]{1,0:T(8,128)(2,1)}) custom-call(s32[16]{0:T(128)} %and_select_fusion.wst, s32[160]{0:T(256)} %select_reduce_fusion.2.chunk, bf16[4096,768]{1,0:T(8,128)(2,1)} %get-tuple-element.78.x_ref, s32[4096,1]{1,0:T(8,128)} %add.223.posc_ref, bf16[5,768,3072]{2,1,0:T(8,128)(2,1)} %up_ref.17, ...), custom_call_target="tpu_custom_call" | custom-call | flops 48318382080 | bytes 30000000 | tf_op jit(solution)/shard_map/fwd/pallas_call | solution.py:265
  1337.7 90.4 %bwd.4.c_ref = bf16[4096,768]{1,0:T(8,128)(2,1)} custom-call(bf16[4096,768]{1,0:T(8,128)(2,1)} %get-tuple-element.78.x_ref, bf16[4096,768]{1,0:T(8,128)(2,1)} %gather_fusion.3, bf16[4096,768]{1,0:T(8,128)(2,1)} %get-tuple-element.83.s_ref, bf16[4096,768]{1,0:T(8,128)(2,1)} %get-tuple-element.84.e_ref, bf16[5,768,3072]{2,1,0:T(8,128)(2,1)} %up_ref.17, ...), custom_call_target="tpu_custom_call" | custom-call | flops 67645734912 | bytes 40000000 | tf_op jit(solution)/shard_map/bwd/pallas_call | solution.py:290
  1460.3 90.3 %bwd.5.c_ref = bf16[4096,768]{1,0:T(8,128)(2,1)} custom-call(bf16[4096,768]{1,0:T(8,128)(2,1)} %get-tuple-element.76.x_ref, bf16[4096,768]{1,0:T(8,128)(2,1)} %bwd.4.c_ref, bf16[4096,768]{1,0:T(8,128)(2,1)} %get-tuple-element.87.s_ref, bf16[4096,768]{1,0:T(8,128)(2,1)} %get-tuple-element.88.e_ref, bf16[5,768,3072]{2,1,0:T(8,128)(2,1)} %up_ref.17, ...), custom_call_target="tpu_custom_call" | custom-call | flops 67645734912 | bytes 40000000 | tf_op jit(solution)/shard_map/bwd/pallas_call | solution.py:290
  1603.4 90.2 %bwd.6.c_ref = bf16[4096,768]{1,0:T(8,128)(2,1)} custom-call(bf16[4096,768]{1,0:T(8,128)(2,1)} %get-tuple-element.70.x_ref, bf16[4096,768]{1,0:T(8,128)(2,1)} %bwd.5.c_ref, bf16[4096,768]{1,0:T(8,128)(2,1)} %get-tuple-element.91.s_ref, bf16[4096,768]{1,0:T(8,128)(2,1)} %get-tuple-element.92.e_ref, bf16[5,768,3072]{2,1,0:T(8,128)(2,1)} %up_ref.17, ...), custom_call_target="tpu_custom_call" | custom-call | flops 67645734912 | bytes 40000000 | tf_op jit(solution)/shard_map/bwd/pallas_call | solution.py:290
  1746.5 90.2 %bwd.7.c_ref = bf16[4096,768]{1,0:T(8,128)(2,1)} custom-call(bf16[4096,768]{1,0:T(8,128)(2,1)} %get-tuple-element.64.x_ref, bf16[4096,768]{1,0:T(8,128)(2,1)} %bwd.6.c_ref, bf16[4096,768]{1,0:T(8,128)(2,1)} %get-tuple-element.95.s_ref, bf16[4096,768]{1,0:T(8,128)(2,1)} %get-tuple-element.96.e_ref, bf16[5,768,3072]{2,1,0:T(8,128)(2,1)} %up_ref.17, ...), custom_call_target="tpu_custom_call" | custom-call | flops 67645734912 | bytes 40000000 | tf_op jit(solution)/shard_map/bwd/pallas_call | solution.py:290
  1918.1 34.1 %scatter.5._ = f32[5,6288,768]{2,1,0:T(8,128)} custom-call(s32[4096]{0:T(1024)} %bitcast.84, s32[8]{0:T(128)} %get-tuple-element.110.count, f32[4096,768]{1,0:T(8,128)} %bitcast.50.recv_ref), custom_call_target="tpu_custom_call" | custom-call | flops 10000000000 | bytes 40000000 | tf_op jit(solution)/shard_map/scatter/pallas_call | solution.py:304
  1952.2 34.1 %scatter.6._ = f32[5,6288,768]{2,1,0:T(8,128)} custom-call(s32[4096]{0:T(1024)} %bitcast.85, s32[8]{0:T(128)} %get-tuple-element.110.count, f32[4096,768]{1,0:T(8,128)} %bitcast.52.recv_ref, f32[5,6288,768]{2,1,0:T(8,128)} %scatter.5._), custom_call_target="tpu_custom_call", output_to_operand_aliasing={{}: (3, {})} | custom-call | flops 10000000000 | bytes 40000000 | tf_op jit(solution)/shard_map/scatter/pallas_call | solution.py:304
  1986.3 34.1 %scatter.7._ = f32[5,6288,768]{2,1,0:T(8,128)} custom-call(s32[4096]{0:T(1024)} %bitcast.86, s32[8]{0:T(128)} %get-tuple-element.110.count, f32[4096,768]{1,0:T(8,128)} %bitcast.54.recv_ref, f32[5,6288,768]{2,1,0:T(8,128)} %scatter.6._), custom_call_target="tpu_custom_call", output_to_operand_aliasing={{}: (3, {})} | custom-call | flops 10000000000 | bytes 40000000 | tf_op jit(solution)/shard_map/scatter/pallas_call | solution.py:304
  2020.4 34.1 %scatter.8._ = f32[5,6288,768]{2,1,0:T(8,128)} custom-call(s32[4096]{0:T(1024)} %bitcast.87, s32[8]{0:T(128)} %get-tuple-element.110.count, f32[4096,768]{1,0:T(8,128)} %bitcast.58.recv_ref, f32[5,6288,768]{2,1,0:T(8,128)} %scatter.7._), custom_call_target="tpu_custom_call", output_to_operand_aliasing={{}: (3, {})} | custom-call | flops 10000000000 | bytes 40000000 | tf_op jit(solution)/shard_map/scatter/pallas_call | solution.py:304
  2054.5 34.2 %scatter.9 = f32[5,6288,768]{2,1,0:T(8,128)} custom-call(s32[4096]{0:T(1024)} %bitcast.88, s32[8]{0:T(128)} %get-tuple-element.110.count, f32[4096,768]{1,0:T(8,128)} %bitcast.56.recv_ref, f32[5,6288,768]{2,1,0:T(8,128)} %scatter.8._), custom_call_target="tpu_custom_call", output_to_operand_aliasing={{}: (3, {})} | custom-call | flops 10000000000 | bytes 40000000 | tf_op jit(solution)/shard_map/scatter/pallas_call | solution.py:304
  (98 shorter events, 360.2 us)
Async XLA Ops:
  0.6 0.7 copy-start
  1.4 48.1 %copy-start.9 = (pred[2560]{0:T(1024)(128)(4,1)S(1)}, pred[2560]{0:T(1024)(128)(4,1)}, u32[]{:S(2)}) copy-start(pred[2560]{0:T(1024)(128)(4,1)} %constant.104.clone.1) | copy-start | bytes 7684
  60.4 8.8 all-to-all-start
  145.4 208.0 %all-to-all-start.1 = ((bf16[8,512,768]{2,1,0:T(8,128)(2,1)}), bf16[8,512,768]{2,1,0:T(8,128)(2,1)}, u32[]{:S(2)}, u32[]{:S(2)}) async-start(bf16[8,512,768]{2,1,0:T(8,128)(2,1)} %bitcast.75), calls=%async_computation.1 | async-start | bytes 12582912 | tf_op jit(solution)/shard_map/all_to_all | solution.py:320
  232.6 211.4 %copy-start.2 = (s32[32,128]{1,0:T(8,128)}, s32[32,128]{1,0:T(8,128)S(1)}, u32[]{:S(2)}) copy-start(s32[32,128]{1,0:T(8,128)S(1)} %reduce-window.25) | copy-start | bytes 49156
  232.8 211.9 %copy-start.4 = (s32[4096]{0:T(1024)}, s32[4096]{0:T(1024)S(1)}, u32[]{:S(2)}) copy-start(s32[4096]{0:T(1024)S(1)} %select_reduce_fusion) | copy-start | bytes 49156
  233.2 74.9 %copy-start.6 = (s32[16,2,128]{2,1,0:T(2,128)}, s32[16,2,128]{2,1,0:T(2,128)S(1)}, u32[]{:S(2)}) copy-start(s32[16,2,128]{2,1,0:T(2,128)S(1)} %broadcast.275) | copy-start | bytes 49156
  353.4 243.4 %all-to-all-start.2 = ((bf16[8,512,768]{2,1,0:T(8,128)(2,1)}), bf16[8,512,768]{2,1,0:T(8,128)(2,1)}, u32[]{:S(2)}, u32[]{:S(2)}) async-start(bf16[8,512,768]{2,1,0:T(8,128)(2,1)} %bitcast.74), calls=%async_computation.2 | async-start | bytes 12582912 | tf_op jit(solution)/shard_map/all_to_all | solution.py:320
  596.8 237.6 %all-to-all-start.3 = ((bf16[8,512,768]{2,1,0:T(8,128)(2,1)}), bf16[8,512,768]{2,1,0:T(8,128)(2,1)}, u32[]{:S(2)}, u32[]{:S(2)}) async-start(bf16[8,512,768]{2,1,0:T(8,128)(2,1)} %bitcast.77), calls=%async_computation.3 | async-start | bytes 12582912 | tf_op jit(solution)/shard_map/all_to_all | solution.py:320
  834.4 237.6 %all-to-all-start.4 = ((bf16[8,512,768]{2,1,0:T(8,128)(2,1)}), bf16[8,512,768]{2,1,0:T(8,128)(2,1)}, u32[]{:S(2)}, u32[]{:S(2)}) async-start(bf16[8,512,768]{2,1,0:T(8,128)(2,1)} %bitcast.78), calls=%async_computation.4 | async-start | bytes 12582912 | tf_op jit(solution)/shard_map/all_to_all | solution.py:320
  1072.1 91.8 %copy-start.3 = (s32[32,128]{1,0:T(8,128)S(1)}, s32[32,128]{1,0:T(8,128)}, u32[]{:S(2)}) copy-start(s32[32,128]{1,0:T(8,128)} %copy-done.2) | copy-start | bytes 49156
  1072.1 91.8 %copy-start.5 = (s32[4096]{0:T(1024)S(1)}, s32[4096]{0:T(1024)}, u32[]{:S(2)}) copy-start(s32[4096]{0:T(1024)} %copy-done.4) | copy-start | bytes 49156
  1072.1 91.8 %copy-start.7 = (s32[16,2,128]{2,1,0:T(2,128)S(1)}, s32[16,2,128]{2,1,0:T(2,128)}, u32[]{:S(2)}) copy-start(s32[16,2,128]{2,1,0:T(2,128)} %copy-done.6) | copy-start | bytes 49156
  1072.1 190.1 %all-to-all-start.5 = ((bf16[8,512,768]{2,1,0:T(8,128)(2,1)}), bf16[8,512,768]{2,1,0:T(8,128)(2,1)}, u32[]{:S(2)}, u32[]{:S(2)}) async-start(bf16[8,512,768]{2,1,0:T(8,128)(2,1)} %bitcast.76), calls=%async_computation.5 | async-start | bytes 12582912 | tf_op jit(solution)/shard_map/all_to_all | solution.py:320
  1262.2 193.0 %all-to-all-start.6 = ((f32[8,512,768]{2,1,0:T(8,128)}), f32[8,512,768]{2,1,0:T(8,128)}, u32[]{:S(2)}, u32[]{:S(2)}) async-start(f32[8,512,768]{2,1,0:T(8,128)} %bitcast.81), calls=%async_computation.6 | async-start | bytes 25165824 | tf_op jit(solution)/shard_map/all_to_all | solution.py:345
  1455.2 144.1 %all-to-all-start.7 = ((f32[8,512,768]{2,1,0:T(8,128)}), f32[8,512,768]{2,1,0:T(8,128)}, u32[]{:S(2)}, u32[]{:S(2)}) async-start(f32[8,512,768]{2,1,0:T(8,128)} %bitcast.82), calls=%async_computation.7 | async-start | bytes 25165824 | tf_op jit(solution)/shard_map/all_to_all | solution.py:345
  1599.3 143.1 %all-to-all-start.8 = ((f32[8,512,768]{2,1,0:T(8,128)}), f32[8,512,768]{2,1,0:T(8,128)}, u32[]{:S(2)}, u32[]{:S(2)}) async-start(f32[8,512,768]{2,1,0:T(8,128)} %bitcast.83), calls=%async_computation.8 | async-start | bytes 25165824 | tf_op jit(solution)/shard_map/all_to_all | solution.py:345
  1742.4 143.0 %all-to-all-start.10 = ((f32[8,512,768]{2,1,0:T(8,128)}), f32[8,512,768]{2,1,0:T(8,128)}, u32[]{:S(2)}, u32[]{:S(2)}) async-start(f32[8,512,768]{2,1,0:T(8,128)} %bitcast.80), calls=%async_computation.10 | async-start | bytes 25165824 | tf_op jit(solution)/shard_map/all_to_all | solution.py:345
  1885.4 4.2 copy-start.8
  1885.4 169.0 %all-to-all-start.9 = ((f32[8,512,768]{2,1,0:T(8,128)}), f32[8,512,768]{2,1,0:T(8,128)}, u32[]{:S(2)}, u32[]{:S(2)}) async-start(f32[8,512,768]{2,1,0:T(8,128)} %bitcast.79), calls=%async_computation.9 | async-start | bytes 25165824 | tf_op jit(solution)/shard_map/all_to_all | solution.py:345
  2054.5 34.2 %copy-start.1 = (s32[2048]{0:T(1024)S(1)}, s32[2048]{0:T(1024)}, u32[]{:S(2)}) copy-start(s32[2048]{0:T(1024)} %param.9) | copy-start | bytes 24580

commit v2 on v1

--- a/solution.py
+++ b/solution.py
@@ -16,6 +16,8 @@
 SUB = 256
 WIN = 384
 TB = 512
+PIECES = 6
+PAD = 16
 FC = 512
 VMEM_LIMIT = 60 * 1024 * 1024
 G0 = 0.7978845608028654
@@ -47,7 +49,7 @@
 
 
 def fwd_kernel(wst, chunk, x_ref, posc_ref, up_ref, dn_ref, gt_ref, pj_ref, ret_ref,
-               xo_ref, e_ref, rows, sem):
+               xo_ref, e_ref, g_ref, rows, sem):
     i = pl.program_id(0)
     n_rows = rows.shape[0]
 
@@ -74,6 +76,7 @@
     e = jnp.concatenate(parts, axis=0)
     e_ref[...] = e
     g = gelu(dot(u, gt_ref[0])).astype(BF16)
+    g_ref[...] = g
     z = (g.astype(F32) * e.astype(F32)).astype(BF16)
     proj = dot(z, pj_ref[0]).astype(BF16)
     ff = up_ref.shape[2]
@@ -85,8 +88,17 @@
     xo_ref[...] = (xf + mlp.astype(BF16).astype(F32) + proj.astype(F32)).astype(BF16)
 
 
-def rowgrad_kernel(wst, chunk, total, x_ref, c_ref, posr_ref, gt_ref, pj_ref,
-                   s_ref, send_ref, acc, sem):
+def rowgrad_top_kernel(wst, chunk, total, x_ref, c_ref, posr_ref, gt_ref, pj_ref, *refs):
+    u = norm_rows(x_ref[...].astype(F32))[0].astype(BF16)
+    g = gelu(dot(u, gt_ref[0])).astype(BF16)
+    rowgrad_body(wst, chunk, total, g, c_ref, posr_ref, pj_ref, *refs)
+
+
+def rowgrad_kernel(wst, chunk, total, g_ref, c_ref, posr_ref, pj_ref, *refs):
+    rowgrad_body(wst, chunk, total, g_ref[...], c_ref, posr_ref, pj_ref, *refs)
+
+
+def rowgrad_body(wst, chunk, total, g, c_ref, posr_ref, pj_ref, s_ref, send_ref, acc, sem):
     i = pl.program_id(0)
     last = pl.num_programs(0) - 1
 
@@ -94,9 +106,7 @@
     def _():
         acc[...] = jnp.zeros_like(acc)
 
-    tb = x_ref.shape[0]
-    u = norm_rows(x_ref[...].astype(F32))[0].astype(BF16)
-    g = gelu(dot(u, gt_ref[0])).astype(BF16)
+    tb = c_ref.shape[0]
     s = dot_nt(c_ref[...], pj_ref[0]).astype(BF16)
     s_ref[...] = s
     k = g.astype(F32) * s.astype(F32)
@@ -147,38 +157,112 @@
     co_ref[...] = (c.astype(F32) + dx).astype(BF16)
 
 
-def scatter_body(layer, row_of, count, recv_ref, out_ref, acc, sem):
+def line_of(row):
+    return (row // 8) * (8 * PIECES) + row % 8
+
+
+def piece_rows(start):
+    return pl.ds(start, PIECES, stride=8)
+
+
+def gather_kernel(steps, line, src_ref, out_ref, table, stage):
     i = pl.program_id(0)
-    cap = recv_ref.shape[0]
+    src_rows = src_ref.shape[1]
+    out_rows = out_ref.shape[0]
+    span = CH * PIECES
+
+    @pl.when(i < steps)
+    def _():
+        def widen(t, carry):
+            blk = src_ref[0, pl.ds(pl.multiple_of(t * CH, CH), CH), :].astype(F32)
+            base = pl.multiple_of((i * src_rows + t * CH) * PIECES, 8)
+            for h in range(CH // 8):
+                for j in range(PIECES):
+                    table[pl.ds(base + (h * PIECES + j) * 8, 8), :] = blk[h * 8:h * 8 + 8, j * 128:j * 128 + 128]
+            return carry
+
+        lax.fori_loop(0, src_rows // CH, widen, 0, unroll=2)
+
+    @pl.when(i >= steps)
+    def _():
+        first = (i - steps) * out_rows
+
+        def pick(t, carry):
+            base = pl.multiple_of(t * (8 * PIECES), 8)
+            got = [table[piece_rows(line[first + t * 8 + q]), :] for q in range(8)]
+            for q, v in enumerate(got):
+                stage[piece_rows(base + q), :] = v
+            return carry
+
+        lax.fori_loop(0, out_rows // 8, pick, 0, unroll=2)
+
+        def narrow(t, carry):
+            base = pl.multiple_of(t * span, 8)
+            halves = [
+                jnp.concatenate([stage[pl.ds(base + (h * PIECES + j) * 8, 8), :] for j in range(PIECES)], axis=1)
+                for h in range(CH // 8)]
+            out_ref[pl.ds(pl.multiple_of(t * CH, CH), CH), :] = jnp.concatenate(halves, axis=0).astype(BF16)
+            return carry
+
+        lax.fori_loop(0, out_rows // CH, narrow, 0, unroll=2)
+
+
+def scatter_body(layer, line, count, recv_ref, out_ref, acc, stage, sem):
+    i = pl.program_id(0)
+    span = 8 * PIECES
+    cap = recv_ref.shape[0] // PIECES
+    n_lines = acc.shape[0] - PAD
 
     @pl.when(i == 0)
     def _():
-        acc[...] = jnp.zeros_like(acc)
+        def clear(t, carry):
+            acc[pl.ds(pl.multiple_of(t * span, 8), span), :] = jnp.zeros((span, 128), F32)
+            return carry
+
+        lax.fori_loop(0, n_lines // span, clear, 0, unroll=2)
+
+    def load(t, carry):
+        at = pl.ds(pl.multiple_of(t * span, 8), span)
+        stage[at, :] = recv_ref[at, :]
+        return carry
+
+    groups = (count[i] + 7) // 8
+    lax.fori_loop(0, groups, load, 0)
 
     def group(t, carry):
-        base = pl.multiple_of(t * 8, 8)
-        idx = [row_of[i * cap + base + q] for q in range(8)]
-        old = [acc[pl.ds(r, 1), :] for r in idx]
-        new = [o + recv_ref[pl.ds(base + q, 1), :] for q, o in enumerate(old)]
-        for r, v in zip(idx, new):
-            acc[pl.ds(r, 1), :] = v
+        base = pl.multiple_of(t * span, 8)
+        at = [line[i * cap + t * 8 + q] for q in range(8)]
+        old = [acc[piece_rows(r), :] for r in at]
+        new = [o + stage[piece_rows(base + q), :] for q, o in enumerate(old)]
+        for r, v in zip(at, new):
+            acc[piece_rows(r), :] = v
         return carry
 
-    lax.fori_loop(0, (count[i] + 7) // 8, group, 0)
+    lax.fori_loop(0, groups, group, 0)
 
     @pl.when(i == pl.num_programs(0) - 1)
     def _():
-        cp = pltpu.make_async_copy(acc.at[pl.ds(0, out_ref.shape[1])], out_ref.at[layer], sem)
+        size = n_lines - span
+        cp = pltpu.make_async_copy(acc.at[pl.ds(0, size)], out_ref.at[pl.ds(layer * size, size)], sem)
         cp.start()
         cp.wait()
 
 
-def scatter_first(layer, row_of, count, recv_ref, out_ref, acc, sem):
-    scatter_body(layer, row_of, count, recv_ref, out_ref, acc, sem)
-
-
-def scatter_next(layer, row_of, count, recv_ref, _, out_ref, acc, sem):
-    scatter_body(layer, row_of, count, recv_ref, out_ref, acc, sem)
+def scatter_first(layer, line, count, recv_ref, *refs):
+    scatter_body(layer, line, count, recv_ref, *refs)
+
+
+def scatter_next(layer, line, count, recv_ref, _, *refs):
+    scatter_body(layer, line, count, recv_ref, *refs)
+
+
+def to_lines(a):
+    n, d = a.shape
+    return a.reshape(n // 8, 8, d // 128, 128).transpose(0, 2, 1, 3).reshape(n * d // 128, 128)
+
+
+def from_lines(a, n, d):
+    return a.reshape(n // 8, d // 128, 8, 128).transpose(0, 2, 1, 3).reshape(n, d)
 
 
 ANY = pl.BlockSpec(memory_space=pl.ANY)
@@ -212,7 +296,12 @@
         my_dev = lax.axis_index('emb')
 
         iota = jnp.arange(n_tok, dtype=I32)
-        tok_id = uniq_loc.at[inv_loc].get(mode='promise_in_bounds')
+        low = 64
+        hot = (inv_loc[:, None] // low == jnp.arange(n_uniq // low, dtype=I32)[None, :]).astype(BF16)
+        grid_ids = uniq_loc.reshape(n_uniq // low, low)
+        near = dot(hot, (grid_ids // 256).astype(BF16)) * 256.0 + dot(hot, (grid_ids % 256).astype(BF16))
+        mine = inv_loc[:, None] % low == jnp.arange(low, dtype=I32)[None, :]
+        tok_id = jnp.sum(jnp.where(mine, near, 0.0), axis=1).astype(I32)
         order = lax.sort(tok_id * n_tok + iota)
         perm = order % n_tok
         sid = order // n_tok
@@ -243,11 +332,11 @@
         valid = recv_ids >= 0
         local_row = recv_ids - my_dev * shard_rows
         fetch_row = jnp.where(valid, local_row, 0).reshape(-1)
-        add_row = jnp.where(valid, local_row, shard_rows).reshape(-1)
+        add_line = line_of(jnp.where(valid, local_row, shard_rows).reshape(-1))
+        fetch_line = line_of(fetch_row)
         add_cnt = jnp.sum(valid.astype(I32), axis=1).astype(I32)
         posc = pos.reshape(n_tok, 1)
         posr = pos.reshape(n_tok // SUB, 1, SUB)
-        flat_tab = tab_loc.reshape(layers * shard_rows, d_emb)
 
         tok_spec = pl.BlockSpec((TB, d_model), lambda i, *_: (i, 0))
         posr_spec = pl.BlockSpec((TB // SUB, 1, SUB), lambda i, *_: (i, 0, 0))
@@ -263,28 +352,29 @@
 
         def forward(layer, x, returned):
             return pl.pallas_call(
-                fwd_kernel, out_shape=[tok_out, tok_out],
+                fwd_kernel, out_shape=[tok_out] * 3,
                 grid_spec=pltpu.PrefetchScalarGridSpec(
                     num_scalar_prefetch=2, grid=grid,
                     in_specs=[tok_spec, pl.BlockSpec((TB, 1), lambda i, *_: (i, 0)),
                               *w_specs(layer, s_up, s_dn, s_sq, s_sq), ANY],
-                    out_specs=[tok_spec, tok_spec],
+                    out_specs=[tok_spec] * 3,
                     scratch_shapes=[pltpu.VMEM((n_rows, d_emb), BF16), pltpu.SemaphoreType.DMA]),
                 compiler_params=params(), name='fwd',
                 cost_estimate=cost(2 * mm + 2 * sq, 3e7),
             )(wst, chunk, x, posc, w_up, w_down, w_gate, w_proj, returned)
 
-        def rowgrad(layer, x, c):
+        def rowgrad(layer, kernel, operand, c, gate):
+            weights = [w_gate] * gate + [w_proj]
             return pl.pallas_call(
-                rowgrad_kernel, out_shape=[tok_out, jax.ShapeDtypeStruct((slots, d_emb), F32)],
+                kernel, out_shape=[tok_out, jax.ShapeDtypeStruct((slots, d_emb), F32)],
                 grid_spec=pltpu.PrefetchScalarGridSpec(
                     num_scalar_prefetch=3, grid=grid,
-                    in_specs=[tok_spec, tok_spec, posr_spec, *w_specs(layer, s_sq, s_sq)],
+                    in_specs=[tok_spec, tok_spec, posr_spec, *w_specs(layer, *[s_sq] * len(weights))],
                     out_specs=[tok_spec, ANY],
                     scratch_shapes=[pltpu.VMEM((n_rows, d_emb), F32), pltpu.SemaphoreType.DMA]),
                 compiler_params=params(), name='rowgrad',
                 cost_estimate=cost(2 * sq, 3e7),
-            )(wst, chunk, total, x, c, posr, w_gate, w_proj)
+            )(wst, chunk, total, operand, c, posr, *weights)
 
         def backward(layer, x, c, s, e):
             return pl.pallas_call(
@@ -296,36 +386,56 @@
             )(x, c, s, e, w_up, w_down, w_gate)
 
         def scatter(layer, received, grads):
-            ins = [pl.BlockSpec((capacity, d_emb), lambda i, *_: (i, 0))]
-            args = [received]
+            ins = [pl.BlockSpec((capacity * PIECES, 128), lambda i, *_: (i, 0))]
+            args = [to_lines(received)]
             if grads is not None:
                 ins.append(ANY)
                 args.append(grads)
             return pl.pallas_call(
                 functools.partial(scatter_first if grads is None else scatter_next, layer),
-                out_shape=jax.ShapeDtypeStruct((layers, shard_rows, d_emb), F32),
+                out_shape=jax.ShapeDtypeStruct((layers * shard_rows * PIECES, 128), F32),
                 grid_spec=pltpu.PrefetchScalarGridSpec(
                     num_scalar_prefetch=2, grid=(group_size,), in_specs=ins, out_specs=ANY,
-                    scratch_shapes=[pltpu.VMEM((shard_rows + 8, d_emb), F32), pltpu.SemaphoreType.DMA]),
+                    scratch_shapes=[pltpu.VMEM(((shard_rows + 8) * PIECES + PAD, 128), F32),
+                                    pltpu.VMEM((capacity * PIECES + PAD, 128), F32), pltpu.SemaphoreType.DMA]),
                 compiler_params=params(), name='scatter',
                 input_output_aliases={} if grads is None else {3: 0},
                 cost_estimate=cost(1e10, 4e7),
-            )(add_row, add_cnt, *args)
-
-        def serve(layer, index):
-            rows = flat_tab.at[index + layer * shard_rows].get(mode='promise_in_bounds')
-            return rows.reshape(group_size, capacity, d_emb)
+            )(add_line, add_cnt, *args)
+
+        def gather(source, layer, line, src_rows, name):
+            n = source.shape[1]
+            steps = n // src_rows
+            return pl.pallas_call(
+                functools.partial(gather_kernel, steps),
+                out_shape=jax.ShapeDtypeStruct((line.shape[0], d_emb), BF16),
+                grid_spec=pltpu.PrefetchScalarGridSpec(
+                    num_scalar_prefetch=1, grid=(steps + line.shape[0] // TB,),
+                    in_specs=[pl.BlockSpec((1, src_rows, d_emb),
+                                           lambda i, *_: (layer, jnp.minimum(i, steps - 1), 0))],
+                    out_specs=pl.BlockSpec((TB, d_emb), lambda i, *_: (jnp.maximum(i - steps, 0), 0)),
+                    scratch_shapes=[pltpu.VMEM((n * PIECES + PAD, 128), F32),
+                                    pltpu.VMEM((TB * PIECES + PAD, 128), F32)]),
+                compiler_params=params(), name=name,
+                cost_estimate=cost(1e10, 2e7),
+            )(line, source)
+
+        def tok_gather(a, rows, name):
+            return gather(a.reshape(1, n_tok, d_model), 0, line_of(rows), n_tok // 4, name)
+
+        def serve(layer, line):
+            return gather(tab_loc, layer, line, shard_rows // 3, 'serve').reshape(group_size, capacity, d_emb)
 
         def exchange(a):
             return lax.all_to_all(a, 'emb', 0, 0)
 
-        served = serve(0, fetch_row)
+        served = serve(0, fetch_line)
         got = exchange(served)
-        perm, served, later = lax.optimization_barrier((perm, served, fetch_row))
-        x = x_loc.at[perm].get(mode='promise_in_bounds')
-        c = dy_loc.at[perm].get(mode='promise_in_bounds')
+        perm, served, later = lax.optimization_barrier((perm, served, fetch_line))
+        x = tok_gather(x_loc, perm, 'sort_x')
+        c = tok_gather(dy_loc, perm, 'sort_c')
         served = serve(1, later)
-        saved_x, saved_e = [], []
+        saved_x, saved_e, saved_g = [], [], []
         for layer in range(layers):
             here = got
             if layer + 1 < layers:
@@ -334,14 +444,18 @@
                 if layer + 2 < layers:
                     served = serve(layer + 2, later)
             saved_x.append(x)
-            x, e = forward(layer, x, here.reshape(slots, d_emb))
+            x, e, g = forward(layer, x, here.reshape(slots, d_emb))
             saved_e.append(e)
-        x_out = x.at[unperm].get(mode='promise_in_bounds')
+            saved_g.append(g)
+        x_out = tok_gather(x, unperm, 'unsort')
 
         grads = None
         pending = None
         for layer in reversed(range(layers)):
-            s, send = rowgrad(layer, saved_x[layer], c)
+            if layer == layers - 1:
+                s, send = rowgrad(layer, rowgrad_top_kernel, saved_x[layer], c, 1)
+            else:
+                s, send = rowgrad(layer, rowgrad_kernel, saved_g[layer], c, 0)
             got = lax.all_to_all(send.reshape(group_size, capacity, d_emb), 'emb', 0, 0).reshape(slots, d_emb)
             if pending is not None:
                 c, pending = lax.optimization_barrier((c, pending))
@@ -350,7 +464,7 @@
                 c = backward(layer, saved_x[layer], c, s, saved_e[layer])
             pending = got
         grads = scatter(0, pending, grads)
-        return x_out, grads
+        return x_out, from_lines(grads, layers * shard_rows, d_emb).reshape(layers, shard_rows, d_emb)
 
     return jax.shard_map(body, mesh=mesh,
                          in_specs=(P('emb'), P('emb'), P('emb', None), P('emb', None), P(None, 'emb', None),

time: 2100 us -> 1320 us (0.63)
  local copies, waits for them, and re-layouts: 470 us -> 5.8 us
  starting transfers between devices: 480 us -> 47.1 us
  waiting for transfers between devices: 68.6 us -> 129 us
  Pallas kernels: 1020 us -> 1080 us
    gather x9 -> x0, local copies, waits for them, and re-layouts: 465 us -> none  [the longest x5 374 us: serve(): rows = flat_tab.at[index + layer * shard_rows].get(mode='promise_in_bounds')]
    all_to_all x5, starting transfers between devices: 453 us -> 20.5 us  [exchange(): return lax.all_to_all(a, 'emb', 0, 0)]
    pallas_call x10 -> x18, Pallas kernels: 490 us -> 591 us  [the longest x5 353 us: forward(): pl.pallas_call(fwd_kernel, out_shape=[tok_out] * 3, grid_spec=pltpu.Prefe...]
    pallas_call x5, Pallas kernels: 170 us -> 126 us  [scatter(): pl.pallas_call(functools.partial(scatter_first if grads is None else scat...]
    all_to_all x5, waiting for transfers between devices: 64 us -> 99.9 us  [body(): lax.all_to_all(send.reshape(group_size, capacity, d_emb), 'emb', 0, 0)]
    all_to_all x5, waiting for transfers between devices: 0.01 us -> 24.2 us  [exchange(): return lax.all_to_all(a, 'emb', 0, 0)]
  transfers between devices with their start and end apart: 11 -> 11, of which waited for: 4 -> 6; matrix products, arithmetic and copies ran while one was open for 18% -> 1% of each run, Pallas kernels for 47% -> 79%
where the time goes in v2:
time: 1320 us; the launch traced here: 1310 us
  Pallas kernels  1080 us (82%)
  waiting for transfers between devices  129 us (10%)
  starting transfers between devices  47.1 us (4%)
  other arithmetic  35.3 us (3%)
  between operations  16.3 us (1%)
    pallas_call x4, Pallas kernels, backward(): pl.pallas_call(bwd_kernel, out_shape=tok_out, grid=grid, in_specs=[tok_sp...  361 us
    pallas_call x5, Pallas kernels, forward(): pl.pallas_call(fwd_kernel, out_shape=[tok_out] * 3, grid_spec=pltpu.Prefe...  353 us
    pallas_call x5, Pallas kernels, scatter(): pl.pallas_call(functools.partial(scatter_first if grads is None else scat...  126 us
    pallas_call x8, Pallas kernels, gather(): pl.pallas_call(functools.partial(gather_kernel, steps), out_shape=jax.Sha...  123 us
    pallas_call x5, Pallas kernels, rowgrad(): pl.pallas_call(kernel, out_shape=[tok_out, jax.ShapeDtypeStruct((slots, d...  115 us
    all_to_all x5, waiting for transfers between devices, body(): lax.all_to_all(send.reshape(group_size, capacity, d_emb), 'emb', 0, 0)  99.9 us
  transfers between devices with their start and end apart: 11, of which 6 were waited for; matrix products, arithmetic and copies ran while one was open for 1% of the time, Pallas kernels for 79%

profile of v2, /device:TPU:0, one launch (start us, length us, event | category | flops | bytes accessed | tf_op | source)
XLA Modules:
  0.0 1312.2 jit_solution(13776007492534650810)
XLA Ops:
  116.8 24.2 %all-to-all-done.1 = bf16[8,512,768]{2,1,0:T(8,128)(2,1)} async-done(((bf16[8,512,768]{2,1,0:T(8,128)(2,1)}), bf16[8,512,768]{2,1,0:T(8,128)(2,1)}, u32[]{:S(2)}, u32[]{:S(2)}) %all-to-all-start.1) | async-done | bytes 6291488 | tf_op jit(solution)/shard_map/all_to_all | solution.py:430
  167.1 70.7 %fwd.5 = (bf16[4096,768]{1,0:T(8,128)(2,1)}, bf16[4096,768]{1,0:T(8,128)(2,1)}, bf16[4096,768]{1,0:T(8,128)(2,1)}) custom-call(s32[16]{0:T(128)} %and_select_fusion.wst, s32[160]{0:T(256)} %select_reduce_fusion.2.chunk, bf16[4096,768]{1,0:T(8,128)(2,1)} %sort_x.1.x_ref, s32[4096,1]{1,0:T(8,128)} %add.208.posc_ref, bf16[5,768,3072]{2,1,0:T(8,128)(2,1)} %up_ref.17, ...), custom_call_target="tpu_custom_call" | custom-call | flops 48318382080 | bytes 30000000 | tf_op jit(solution)/shard_map/fwd/pallas_call | solution.py:354
  257.7 70.7 %fwd.6 = (bf16[4096,768]{1,0:T(8,128)(2,1)}, bf16[4096,768]{1,0:T(8,128)(2,1)}, bf16[4096,768]{1,0:T(8,128)(2,1)}) custom-call(s32[16]{0:T(128)} %and_select_fusion.wst, s32[160]{0:T(256)} %select_reduce_fusion.2.chunk, bf16[4096,768]{1,0:T(8,128)(2,1)} %get-tuple-element.69.x_ref, s32[4096,1]{1,0:T(8,128)} %add.208.posc_ref, bf16[5,768,3072]{2,1,0:T(8,128)(2,1)} %up_ref.17, ...), custom_call_target="tpu_custom_call" | custom-call | flops 48318382080 | bytes 30000000 | tf_op jit(solution)/shard_map/fwd/pallas_call | solution.py:354
  348.5 70.7 %fwd.7 = (bf16[4096,768]{1,0:T(8,128)(2,1)}, bf16[4096,768]{1,0:T(8,128)(2,1)}, bf16[4096,768]{1,0:T(8,128)(2,1)}) custom-call(s32[16]{0:T(128)} %and_select_fusion.wst, s32[160]{0:T(256)} %select_reduce_fusion.2.chunk, bf16[4096,768]{1,0:T(8,128)(2,1)} %get-tuple-element.75.x_ref, s32[4096,1]{1,0:T(8,128)} %add.208.posc_ref, bf16[5,768,3072]{2,1,0:T(8,128)(2,1)} %up_ref.17, ...), custom_call_target="tpu_custom_call" | custom-call | flops 48318382080 | bytes 30000000 | tf_op jit(solution)/shard_map/fwd/pallas_call | solution.py:354
  424.8 70.6 %fwd.8 = (bf16[4096,768]{1,0:T(8,128)(2,1)}, bf16[4096,768]{1,0:T(8,128)(2,1)}, bf16[4096,768]{1,0:T(8,128)(2,1)}) custom-call(s32[16]{0:T(128)} %and_select_fusion.wst, s32[160]{0:T(256)} %select_reduce_fusion.2.chunk, bf16[4096,768]{1,0:T(8,128)(2,1)} %get-tuple-element.81.x_ref, s32[4096,1]{1,0:T(8,128)} %add.208.posc_ref, bf16[5,768,3072]{2,1,0:T(8,128)(2,1)} %up_ref.17, ...), custom_call_target="tpu_custom_call" | custom-call | flops 48318382080 | bytes 30000000 | tf_op jit(solution)/shard_map/fwd/pallas_call | solution.py:354
  495.4 30.7 %rowgrad.5 = (bf16[4096,768]{1,0:T(8,128)(2,1)}, f32[4096,768]{1,0:T(8,128)}) custom-call(s32[16]{0:T(128)} %and_select_fusion.wst, s32[160]{0:T(256)} %select_reduce_fusion.2.chunk, s32[1]{0:T(128)} %bitcast.45.total, bf16[4096,768]{1,0:T(8,128)(2,1)} %get-tuple-element.83.x_ref, bf16[4096,768]{1,0:T(8,128)(2,1)} %sort_c.1.c_ref, ...), custom_call_target="tpu_custom_call" | custom-call | flops 9663676416 | bytes 30000000 | tf_op jit(solution)/shard_map/rowgrad/pallas_call | solution.py:368
  530.6 70.6 %fwd.9 = (bf16[4096,768]{1,0:T(8,128)(2,1)}, bf16[4096,768]{1,0:T(8,128)(2,1)}, bf16[4096,768]{1,0:T(8,128)(2,1)}) custom-call(s32[16]{0:T(128)} %and_select_fusion.wst, s32[160]{0:T(256)} %select_reduce_fusion.2.chunk, bf16[4096,768]{1,0:T(8,128)(2,1)} %get-tuple-element.83.x_ref, s32[4096,1]{1,0:T(8,128)} %add.208.posc_ref, bf16[5,768,3072]{2,1,0:T(8,128)(2,1)} %up_ref.17, ...), custom_call_target="tpu_custom_call" | custom-call | flops 48318382080 | bytes 30000000 | tf_op jit(solution)/shard_map/fwd/pallas_call | solution.py:354
  601.2 90.8 %bwd.4.c_ref = bf16[4096,768]{1,0:T(8,128)(2,1)} custom-call(bf16[4096,768]{1,0:T(8,128)(2,1)} %get-tuple-element.83.x_ref, bf16[4096,768]{1,0:T(8,128)(2,1)} %sort_c.1.c_ref, bf16[4096,768]{1,0:T(8,128)(2,1)} %get-tuple-element.88.s_ref, bf16[4096,768]{1,0:T(8,128)(2,1)} %get-tuple-element.89.e_ref, bf16[5,768,3072]{2,1,0:T(8,128)(2,1)} %up_ref.17, ...), custom_call_target="tpu_custom_call" | custom-call | flops 67645734912 | bytes 40000000 | tf_op jit(solution)/shard_map/bwd/pallas_call | solution.py:380
  692.0 21.0 %rowgrad.6 = (bf16[4096,768]{1,0:T(8,128)(2,1)}, f32[4096,768]{1,0:T(8,128)}) custom-call(s32[16]{0:T(128)} %and_select_fusion.wst, s32[160]{0:T(256)} %select_reduce_fusion.2.chunk, s32[1]{0:T(128)} %bitcast.45.total, bf16[4096,768]{1,0:T(8,128)(2,1)} %get-tuple-element.92.g_ref, bf16[4096,768]{1,0:T(8,128)(2,1)} %bwd.4.c_ref, ...), custom_call_target="tpu_custom_call" | custom-call | flops 9663676416 | bytes 30000000 | tf_op jit(solution)/shard_map/rowgrad/pallas_call | solution.py:368
  717.9 90.2 %bwd.5.c_ref = bf16[4096,768]{1,0:T(8,128)(2,1)} custom-call(bf16[4096,768]{1,0:T(8,128)(2,1)} %get-tuple-element.81.x_ref, bf16[4096,768]{1,0:T(8,128)(2,1)} %bwd.4.c_ref, bf16[4096,768]{1,0:T(8,128)(2,1)} %get-tuple-element.93.s_ref, bf16[4096,768]{1,0:T(8,128)(2,1)} %get-tuple-element.94.e_ref, bf16[5,768,3072]{2,1,0:T(8,128)(2,1)} %up_ref.17, ...), custom_call_target="tpu_custom_call" | custom-call | flops 67645734912 | bytes 40000000 | tf_op jit(solution)/shard_map/bwd/pallas_call | solution.py:380
  808.1 21.0 %rowgrad.7 = (bf16[4096,768]{1,0:T(8,128)(2,1)}, f32[4096,768]{1,0:T(8,128)}) custom-call(s32[16]{0:T(128)} %and_select_fusion.wst, s32[160]{0:T(256)} %select_reduce_fusion.2.chunk, s32[1]{0:T(128)} %bitcast.45.total, bf16[4096,768]{1,0:T(8,128)(2,1)} %get-tuple-element.97.g_ref, bf16[4096,768]{1,0:T(8,128)(2,1)} %bwd.5.c_ref, ...), custom_call_target="tpu_custom_call" | custom-call | flops 9663676416 | bytes 30000000 | tf_op jit(solution)/shard_map/rowgrad/pallas_call | solution.py:368
  829.1 27.8 %all-to-all-done.7 = f32[8,512,768]{2,1,0:T(8,128)} async-done(((f32[8,512,768]{2,1,0:T(8,128)}), f32[8,512,768]{2,1,0:T(8,128)}, u32[]{:S(2)}, u32[]{:S(2)}) %all-to-all-start.7) | async-done | bytes 12582944 | tf_op jit(solution)/shard_map/all_to_all | solution.py:459
  861.5 90.2 %bwd.6.c_ref = bf16[4096,768]{1,0:T(8,128)(2,1)} custom-call(bf16[4096,768]{1,0:T(8,128)(2,1)} %get-tuple-element.75.x_ref, bf16[4096,768]{1,0:T(8,128)(2,1)} %bwd.5.c_ref, bf16[4096,768]{1,0:T(8,128)(2,1)} %get-tuple-element.98.s_ref, bf16[4096,768]{1,0:T(8,128)(2,1)} %get-tuple-element.99.e_ref, bf16[5,768,3072]{2,1,0:T(8,128)(2,1)} %up_ref.17, ...), custom_call_target="tpu_custom_call" | custom-call | flops 67645734912 | bytes 40000000 | tf_op jit(solution)/shard_map/bwd/pallas_call | solution.py:380
  951.7 21.1 %rowgrad.8 = (bf16[4096,768]{1,0:T(8,128)(2,1)}, f32[4096,768]{1,0:T(8,128)}) custom-call(s32[16]{0:T(128)} %and_select_fusion.wst, s32[160]{0:T(256)} %select_reduce_fusion.2.chunk, s32[1]{0:T(128)} %bitcast.45.total, bf16[4096,768]{1,0:T(8,128)(2,1)} %get-tuple-element.102.g_ref, bf16[4096,768]{1,0:T(8,128)(2,1)} %bwd.6.c_ref, ...), custom_call_target="tpu_custom_call" | custom-call | flops 9663676416 | bytes 30000000 | tf_op jit(solution)/shard_map/rowgrad/pallas_call | solution.py:368
  972.8 27.7 %all-to-all-done.8 = f32[8,512,768]{2,1,0:T(8,128)} async-done(((f32[8,512,768]{2,1,0:T(8,128)}), f32[8,512,768]{2,1,0:T(8,128)}, u32[]{:S(2)}, u32[]{:S(2)}) %all-to-all-start.8) | async-done | bytes 12582944 | tf_op jit(solution)/shard_map/all_to_all | solution.py:459
  1004.7 90.2 %bwd.7.c_ref = bf16[4096,768]{1,0:T(8,128)(2,1)} custom-call(bf16[4096,768]{1,0:T(8,128)(2,1)} %get-tuple-element.69.x_ref, bf16[4096,768]{1,0:T(8,128)(2,1)} %bwd.6.c_ref, bf16[4096,768]{1,0:T(8,128)(2,1)} %get-tuple-element.103.s_ref, bf16[4096,768]{1,0:T(8,128)(2,1)} %get-tuple-element.104.e_ref, bf16[5,768,3072]{2,1,0:T(8,128)(2,1)} %up_ref.17, ...), custom_call_target="tpu_custom_call" | custom-call | flops 67645734912 | bytes 40000000 | tf_op jit(solution)/shard_map/bwd/pallas_call | solution.py:380
  1094.9 21.0 %rowgrad.9 = (bf16[4096,768]{1,0:T(8,128)(2,1)}, f32[4096,768]{1,0:T(8,128)}) custom-call(s32[16]{0:T(128)} %and_select_fusion.wst, s32[160]{0:T(256)} %select_reduce_fusion.2.chunk, s32[1]{0:T(128)} %bitcast.45.total, bf16[4096,768]{1,0:T(8,128)(2,1)} %get-tuple-element.86.g_ref, bf16[4096,768]{1,0:T(8,128)(2,1)} %bwd.7.c_ref, ...), custom_call_target="tpu_custom_call" | custom-call | flops 9663676416 | bytes 30000000 | tf_op jit(solution)/shard_map/rowgrad/pallas_call | solution.py:368
  1115.9 27.8 %all-to-all-done.10 = f32[8,512,768]{2,1,0:T(8,128)} async-done(((f32[8,512,768]{2,1,0:T(8,128)}), f32[8,512,768]{2,1,0:T(8,128)}, u32[]{:S(2)}, u32[]{:S(2)}) %all-to-all-start.10) | async-done | bytes 12582944 | tf_op jit(solution)/shard_map/all_to_all | solution.py:459
  1169.5 25.2 %scatter.5._ = f32[188640,128]{1,0:T(8,128)} custom-call(s32[4096]{0:T(1024)} %fusion.15.line, s32[8]{0:T(128)} %get-tuple-element.118.count, f32[24576,128]{1,0:T(8,128)} %bitcast.72.recv_ref), custom_call_target="tpu_custom_call" | custom-call | flops 10000000000 | bytes 40000000 | tf_op jit(solution)/shard_map/scatter/pallas_call | solution.py:394
  1194.7 25.2 %scatter.6._ = f32[188640,128]{1,0:T(8,128)} custom-call(s32[4096]{0:T(1024)} %fusion.15.line, s32[8]{0:T(128)} %get-tuple-element.118.count, f32[24576,128]{1,0:T(8,128)} %bitcast.69.recv_ref, f32[188640,128]{1,0:T(8,128)} %scatter.5._), custom_call_target="tpu_custom_call", output_to_operand_aliasing={{}: (3, {})} | custom-call | flops 10000000000 | bytes 40000000 | tf_op jit(solution)/shard_map/scatter/pallas_call | solution.py:394
  1219.9 25.2 %scatter.7._ = f32[188640,128]{1,0:T(8,128)} custom-call(s32[4096]{0:T(1024)} %fusion.15.line, s32[8]{0:T(128)} %get-tuple-element.118.count, f32[24576,128]{1,0:T(8,128)} %bitcast.66.recv_ref, f32[188640,128]{1,0:T(8,128)} %scatter.6._), custom_call_target="tpu_custom_call", output_to_operand_aliasing={{}: (3, {})} | custom-call | flops 10000000000 | bytes 40000000 | tf_op jit(solution)/shard_map/scatter/pallas_call | solution.py:394
  1245.0 25.2 %scatter.8._ = f32[188640,128]{1,0:T(8,128)} custom-call(s32[4096]{0:T(1024)} %fusion.15.line, s32[8]{0:T(128)} %get-tuple-element.118.count, f32[24576,128]{1,0:T(8,128)} %bitcast.63.recv_ref, f32[188640,128]{1,0:T(8,128)} %scatter.7._), custom_call_target="tpu_custom_call", output_to_operand_aliasing={{}: (3, {})} | custom-call | flops 10000000000 | bytes 40000000 | tf_op jit(solution)/shard_map/scatter/pallas_call | solution.py:394
  1270.2 16.7 %all-to-all-done.9 = f32[8,512,768]{2,1,0:T(8,128)} async-done(((f32[8,512,768]{2,1,0:T(8,128)}), f32[8,512,768]{2,1,0:T(8,128)}, u32[]{:S(2)}, u32[]{:S(2)}) %all-to-all-start.9) | async-done | bytes 12582944 | tf_op jit(solution)/shard_map/all_to_all | solution.py:459
  1286.9 25.2 %scatter.9 = f32[188640,128]{1,0:T(8,128)} custom-call(s32[4096]{0:T(1024)} %fusion.15.line, s32[8]{0:T(128)} %get-tuple-element.118.count, f32[24576,128]{1,0:T(8,128)} %bitcast.58.recv_ref, f32[188640,128]{1,0:T(8,128)} %scatter.8._), custom_call_target="tpu_custom_call", output_to_operand_aliasing={{}: (3, {})} | custom-call | flops 10000000000 | bytes 40000000 | tf_op jit(solution)/shard_map/scatter/pallas_call | solution.py:394
  (92 shorter events, 216.5 us)
Async XLA Ops:
  39.3 8.9 all-to-all-start
  65.9 75.0 %all-to-all-start.1 = ((bf16[8,512,768]{2,1,0:T(8,128)(2,1)}), bf16[8,512,768]{2,1,0:T(8,128)(2,1)}, u32[]{:S(2)}, u32[]{:S(2)}) async-start(bf16[8,512,768]{2,1,0:T(8,128)(2,1)} %bitcast.98), calls=%async_computation.1 | async-start | bytes 12582912 | tf_op jit(solution)/shard_map/all_to_all | solution.py:430
  69.7 16.6 %copy-start = (s32[32,128]{1,0:T(8,128)}, s32[32,128]{1,0:T(8,128)S(1)}, u32[]{:S(2)}) copy-start(s32[32,128]{1,0:T(8,128)S(1)} %reduce-window.25) | copy-start | bytes 49156
  69.9 76.1 %copy-start.2 = (s32[4096]{0:T(1024)}, s32[4096]{0:T(1024)S(1)}, u32[]{:S(2)}) copy-start(s32[4096]{0:T(1024)S(1)} %select_reduce_fusion) | copy-start | bytes 49156
  70.3 16.0 %copy-start.4 = (s32[16,2,128]{2,1,0:T(2,128)}, s32[16,2,128]{2,1,0:T(2,128)S(1)}, u32[]{:S(2)}) copy-start(s32[16,2,128]{2,1,0:T(2,128)S(1)} %broadcast.302) | copy-start | bytes 49156
  140.9 96.8 %all-to-all-start.2 = ((bf16[8,512,768]{2,1,0:T(8,128)(2,1)}), bf16[8,512,768]{2,1,0:T(8,128)(2,1)}, u32[]{:S(2)}, u32[]{:S(2)}) async-start(bf16[8,512,768]{2,1,0:T(8,128)(2,1)} %bitcast.99), calls=%async_computation.2 | async-start | bytes 12582912 | tf_op jit(solution)/shard_map/all_to_all | solution.py:430
  237.8 90.6 %all-to-all-start.3 = ((bf16[8,512,768]{2,1,0:T(8,128)(2,1)}), bf16[8,512,768]{2,1,0:T(8,128)(2,1)}, u32[]{:S(2)}, u32[]{:S(2)}) async-start(bf16[8,512,768]{2,1,0:T(8,128)(2,1)} %bitcast.101), calls=%async_computation.3 | async-start | bytes 12582912 | tf_op jit(solution)/shard_map/all_to_all | solution.py:430
  328.4 90.9 %all-to-all-start.4 = ((bf16[8,512,768]{2,1,0:T(8,128)(2,1)}), bf16[8,512,768]{2,1,0:T(8,128)(2,1)}, u32[]{:S(2)}, u32[]{:S(2)}) async-start(bf16[8,512,768]{2,1,0:T(8,128)(2,1)} %bitcast.102), calls=%async_computation.4 | async-start | bytes 12582912 | tf_op jit(solution)/shard_map/all_to_all | solution.py:430
  419.3 4.9 copy-start.1
  419.3 4.9 copy-start.3
  419.3 4.9 copy-start.5
  419.3 106.8 %all-to-all-start.5 = ((bf16[8,512,768]{2,1,0:T(8,128)(2,1)}), bf16[8,512,768]{2,1,0:T(8,128)(2,1)}, u32[]{:S(2)}, u32[]{:S(2)}) async-start(bf16[8,512,768]{2,1,0:T(8,128)(2,1)} %bitcast.100), calls=%async_computation.5 | async-start | bytes 12582912 | tf_op jit(solution)/shard_map/all_to_all | solution.py:430
  526.2 186.9 %all-to-all-start.6 = ((f32[8,512,768]{2,1,0:T(8,128)}), f32[8,512,768]{2,1,0:T(8,128)}, u32[]{:S(2)}, u32[]{:S(2)}) async-start(f32[8,512,768]{2,1,0:T(8,128)} %bitcast.105), calls=%async_computation.6 | async-start | bytes 25165824 | tf_op jit(solution)/shard_map/all_to_all | solution.py:459
  713.0 143.9 %all-to-all-start.7 = ((f32[8,512,768]{2,1,0:T(8,128)}), f32[8,512,768]{2,1,0:T(8,128)}, u32[]{:S(2)}, u32[]{:S(2)}) async-start(f32[8,512,768]{2,1,0:T(8,128)} %bitcast.106), calls=%async_computation.7 | async-start | bytes 25165824 | tf_op jit(solution)/shard_map/all_to_all | solution.py:459
  856.9 143.5 %all-to-all-start.8 = ((f32[8,512,768]{2,1,0:T(8,128)}), f32[8,512,768]{2,1,0:T(8,128)}, u32[]{:S(2)}, u32[]{:S(2)}) async-start(f32[8,512,768]{2,1,0:T(8,128)} %bitcast.107), calls=%async_computation.8 | async-start | bytes 25165824 | tf_op jit(solution)/shard_map/all_to_all | solution.py:459
  1000.4 143.2 %all-to-all-start.10 = ((f32[8,512,768]{2,1,0:T(8,128)}), f32[8,512,768]{2,1,0:T(8,128)}, u32[]{:S(2)}, u32[]{:S(2)}) async-start(f32[8,512,768]{2,1,0:T(8,128)} %bitcast.104), calls=%async_computation.10 | async-start | bytes 25165824 | tf_op jit(solution)/shard_map/all_to_all | solution.py:459
  1143.7 4.2 copy-start.6
  1143.7 10.7 copy-start.7
  1143.7 143.2 %all-to-all-start.9 = ((f32[8,512,768]{2,1,0:T(8,128)}), f32[8,512,768]{2,1,0:T(8,128)}, u32[]{:S(2)}, u32[]{:S(2)}) async-start(f32[8,512,768]{2,1,0:T(8,128)} %bitcast.103), calls=%async_computation.9 | async-start | bytes 25165824 | tf_op jit(solution)/shard_map/all_to_all | solution.py:459

commit v3 on v2

--- a/solution.py
+++ b/solution.py
@@ -6,6 +6,7 @@
 from jax.experimental import pallas as pl
 from jax.experimental.pallas import tpu as pltpu
 from jax.sharding import PartitionSpec as P
+
 
 EPSILON = 1e-6
 BF16 = jnp.bfloat16
@@ -62,7 +63,7 @@
             return carry
 
         lax.fori_loop(0, n_rows // CH, start, 0)
-        pltpu.make_async_copy(ret_ref.at[pl.ds(0, n_rows)], rows, sem).wait()
+        pltpu.make_async_copy(rows, rows, sem).wait()
 
     tb = x_ref.shape[0]
     xf = x_ref[...].astype(F32)
@@ -88,17 +89,17 @@
     xo_ref[...] = (xf + mlp.astype(BF16).astype(F32) + proj.astype(F32)).astype(BF16)
 
 
-def rowgrad_top_kernel(wst, chunk, total, x_ref, c_ref, posr_ref, gt_ref, pj_ref, *refs):
+def rowgrad_top_kernel(wst, dest, total, x_ref, c_ref, posr_ref, gt_ref, pj_ref, *refs):
     u = norm_rows(x_ref[...].astype(F32))[0].astype(BF16)
     g = gelu(dot(u, gt_ref[0])).astype(BF16)
-    rowgrad_body(wst, chunk, total, g, c_ref, posr_ref, pj_ref, *refs)
-
-
-def rowgrad_kernel(wst, chunk, total, g_ref, c_ref, posr_ref, pj_ref, *refs):
-    rowgrad_body(wst, chunk, total, g_ref[...], c_ref, posr_ref, pj_ref, *refs)
-
-
-def rowgrad_body(wst, chunk, total, g, c_ref, posr_ref, pj_ref, s_ref, send_ref, acc, sem):
+    rowgrad_body(wst, dest, total, g, c_ref, posr_ref, pj_ref, *refs)
+
+
+def rowgrad_kernel(wst, dest, total, g_ref, c_ref, posr_ref, pj_ref, *refs):
+    rowgrad_body(wst, dest, total, g_ref[...], c_ref, posr_ref, pj_ref, *refs)
+
+
+def rowgrad_body(wst, dest, total, g, c_ref, posr_ref, pj_ref, s_ref, base_ref, over_ref, rest_ref, acc, sem):
     i = pl.program_id(0)
     last = pl.num_programs(0) - 1
 
@@ -121,17 +122,22 @@
 
     @pl.when(i == last)
     def _():
-        def copy(d):
-            dst = pl.multiple_of(chunk[d] * CH, CH)
-            src = pl.multiple_of(d * CH, CH)
-            return pltpu.make_async_copy(acc.at[pl.ds(src, CH)], send_ref.at[pl.ds(dst, CH)], sem)
+        edges = [0]
+        for ref in (base_ref, over_ref, rest_ref):
+            edges.append(edges[-1] + ref.shape[0] // CH)
 
         def start(d, carry):
-            copy(d).start()
+            src = acc.at[pl.ds(pl.multiple_of(d * CH, CH), CH)]
+            to = dest[d]
+            for ref, low, high in zip((base_ref, over_ref, rest_ref), edges, edges[1:]):
+                @pl.when((to >= low) & (to < high))
+                def _():
+                    dst = ref.at[pl.ds(pl.multiple_of((to - low) * CH, CH), CH)]
+                    pltpu.make_async_copy(src, dst, sem).start()
             return carry
 
         def wait(d, carry):
-            copy(d).wait()
+            pltpu.make_async_copy(acc.at[pl.ds(0, CH)], base_ref.at[pl.ds(0, CH)], sem).wait()
             return carry
 
         lax.fori_loop(0, total[0], start, 0)
@@ -207,11 +213,40 @@
         lax.fori_loop(0, out_rows // CH, narrow, 0, unroll=2)
 
 
-def scatter_body(layer, line, count, recv_ref, out_ref, acc, stage, sem):
+def add_rows(line, at, groups, recv_ref, first, acc, stage):
+    span = 8 * PIECES
+
+    def load(t, carry):
+        src = pl.ds(pl.multiple_of(first + t * span, 8), span)
+        stage[pl.ds(pl.multiple_of(t * span, 8), span), :] = recv_ref[src, :]
+        return carry
+
+    def group(t, carry):
+        base = pl.multiple_of(t * span, 8)
+        to = [line[at + t * 8 + q] for q in range(8)]
+        old = [acc[piece_rows(r), :] for r in to]
+        new = [o + stage[piece_rows(base + q), :] for q, o in enumerate(old)]
+        for r, v in zip(to, new):
+            acc[piece_rows(r), :] = v
+        return carry
+
+    lax.fori_loop(0, groups, load, 0)
+    lax.fori_loop(0, groups, group, 0)
+
+
+def store_layer(layer, out_ref, acc, sem, back=False):
+    size = acc.shape[0] - PAD - 8 * PIECES
+    ends = acc.at[pl.ds(0, size)], out_ref.at[pl.ds(layer * size, size)]
+    cp = pltpu.make_async_copy(ends[1], ends[0], sem) if back else pltpu.make_async_copy(*ends, sem)
+    cp.start()
+    cp.wait()
+
+
+def scatter_kernel(layer, line, n_base, n_over, at_over, base_ref, over_ref, *refs):
+    out_ref, acc, stage, sem = refs[-4:]
     i = pl.program_id(0)
     span = 8 * PIECES
-    cap = recv_ref.shape[0] // PIECES
-    n_lines = acc.shape[0] - PAD
+    cap = base_ref.shape[0] // PIECES + over_ref.shape[0] // PIECES
 
     @pl.when(i == 0)
     def _():
@@ -219,41 +254,29 @@
             acc[pl.ds(pl.multiple_of(t * span, 8), span), :] = jnp.zeros((span, 128), F32)
             return carry
 
-        lax.fori_loop(0, n_lines // span, clear, 0, unroll=2)
-
-    def load(t, carry):
-        at = pl.ds(pl.multiple_of(t * span, 8), span)
-        stage[at, :] = recv_ref[at, :]
-        return carry
-
-    groups = (count[i] + 7) // 8
-    lax.fori_loop(0, groups, load, 0)
-
-    def group(t, carry):
-        base = pl.multiple_of(t * span, 8)
-        at = [line[i * cap + t * 8 + q] for q in range(8)]
-        old = [acc[piece_rows(r), :] for r in at]
-        new = [o + stage[piece_rows(base + q), :] for q, o in enumerate(old)]
-        for r, v in zip(at, new):
-            acc[piece_rows(r), :] = v
-        return carry
-
-    lax.fori_loop(0, groups, group, 0)
+        lax.fori_loop(0, (acc.shape[0] - PAD) // span, clear, 0, unroll=2)
+
+    add_rows(line, i * cap, (n_base[i] + 7) // 8, base_ref, 0, acc, stage)
+    add_rows(line, i * cap + cap // 2, (n_over[i] + 7) // 8, over_ref, at_over[i] * (CH * PIECES), acc, stage)
 
     @pl.when(i == pl.num_programs(0) - 1)
     def _():
-        size = n_lines - span
-        cp = pltpu.make_async_copy(acc.at[pl.ds(0, size)], out_ref.at[pl.ds(layer * size, size)], sem)
-        cp.start()
-        cp.wait()
-
-
-def scatter_first(layer, line, count, recv_ref, *refs):
-    scatter_body(layer, line, count, recv_ref, *refs)
-
-
-def scatter_next(layer, line, count, recv_ref, _, *refs):
-    scatter_body(layer, line, count, recv_ref, *refs)
+        store_layer(layer, out_ref, acc, sem)
+
+
+def rest_kernel(layer, line, n_rest, rest_ref, _, out_ref, acc, stage, sem):
+    i = pl.program_id(0)
+    cap = 2 * rest_ref.shape[0] // PIECES
+
+    @pl.when(i == 0)
+    def _():
+        store_layer(layer, out_ref, acc, sem, back=True)
+
+    add_rows(line, i * cap + cap // 2, (n_rest[i] + 7) // 8, rest_ref, 0, acc, stage)
+
+    @pl.when(i == pl.num_programs(0) - 1)
+    def _():
+        store_layer(layer, out_ref, acc, sem)
 
 
 def to_lines(a):
@@ -322,19 +345,40 @@
         cid = jnp.arange(row_chunks, dtype=I32)[None, :]
         in_own = (cid >= first_ch[:, None]) & (cid < (first_ch + n_ch)[:, None])
         chunk = jnp.sum(jnp.where(in_own, owners[:, None] * cap_ch + cid - first_ch[:, None], 0), axis=0).astype(I32)
+        half_ch = cap_ch // 2
+        over_ch = jnp.maximum(n_ch - half_ch, 0)
+        over_first = (jnp.cumsum(over_ch) - over_ch).astype(I32)
+        fits = over_first + over_ch <= half_ch
+        k_ch = cid - first_ch[:, None]
+        over_dest = jnp.where(fits, group_size * half_ch + over_first - half_ch,
+                              (group_size + 1) * half_ch + (owners - 1) * half_ch)
+        dest = jnp.where(k_ch < half_ch, owners[:, None] * half_ch + k_ch, over_dest[:, None] + k_ch)
+        dest = jnp.sum(jnp.where(in_own, dest, 0), axis=0).astype(I32)
+        unfit = jnp.any(~fits).astype(I32)
         total = jnp.sum(n_ch).astype(I32).reshape(1)
         used_pad = jnp.concatenate([used, jnp.full((capacity,), -1, I32)])
         kk = jnp.arange(capacity, dtype=I32)
         send_ids = jnp.stack([
             jnp.where(kk < cnt[j], lax.dynamic_slice(used_pad, (first[j],), (capacity,)), -1)
             for j in range(group_size)])
-        recv_ids = lax.all_to_all(send_ids, 'emb', 0, 0)
+        notes = jnp.where(jnp.arange(128)[None, :] == 0, over_first[:, None], unfit)
+        mail = lax.all_to_all(jnp.concatenate([send_ids, notes], axis=1), 'emb', 0, 0)
+        recv_ids = mail[:, :capacity]
         valid = recv_ids >= 0
         local_row = recv_ids - my_dev * shard_rows
         fetch_row = jnp.where(valid, local_row, 0).reshape(-1)
         add_line = line_of(jnp.where(valid, local_row, shard_rows).reshape(-1))
         fetch_line = line_of(fetch_row)
-        add_cnt = jnp.sum(valid.astype(I32), axis=1).astype(I32)
+        recv_cnt = jnp.sum(valid.astype(I32), axis=1).astype(I32)
+        half = capacity // 2
+        n_base = jnp.minimum(recv_cnt, half)
+        beyond = jnp.maximum(recv_cnt - half, 0)
+        at_over = mail[:, capacity]
+        fitted = at_over + (beyond + CH - 1) // CH <= half_ch
+        n_over = jnp.where(fitted, beyond, 0)
+        at_over = jnp.where(fitted, at_over, 0)
+        n_rest = jnp.where(fitted, 0, beyond)
+        any_rest = jnp.max(mail[:, capacity + 1])
         posc = pos.reshape(n_tok, 1)
         posr = pos.reshape(n_tok // SUB, 1, SUB)
 
@@ -366,15 +410,15 @@
         def rowgrad(layer, kernel, operand, c, gate):
             weights = [w_gate] * gate + [w_proj]
             return pl.pallas_call(
-                kernel, out_shape=[tok_out, jax.ShapeDtypeStruct((slots, d_emb), F32)],
+                kernel, out_shape=[tok_out] + [jax.ShapeDtypeStruct((r, d_emb), F32) for r in (slots // 2, half, slots // 2)],
                 grid_spec=pltpu.PrefetchScalarGridSpec(
                     num_scalar_prefetch=3, grid=grid,
                     in_specs=[tok_spec, tok_spec, posr_spec, *w_specs(layer, *[s_sq] * len(weights))],
-                    out_specs=[tok_spec, ANY],
+                    out_specs=[tok_spec, ANY, ANY, ANY],
                     scratch_shapes=[pltpu.VMEM((n_rows, d_emb), F32), pltpu.SemaphoreType.DMA]),
                 compiler_params=params(), name='rowgrad',
                 cost_estimate=cost(2 * sq, 3e7),
-            )(wst, chunk, total, operand, c, posr, *weights)
+            )(wst, dest, total, operand, c, posr, *weights)
 
         def backward(layer, x, c, s, e):
             return pl.pallas_call(
@@ -385,25 +429,37 @@
                 cost_estimate=cost(3 * mm + 2 * sq, 4e7),
             )(x, c, s, e, w_up, w_down, w_gate)
 
+        half_spec = pl.BlockSpec((half * PIECES, 128), lambda i, *_: (i, 0))
+        acc_scratch = [pltpu.VMEM(((shard_rows + 8) * PIECES + PAD, 128), F32),
+                       pltpu.VMEM((half * PIECES + PAD, 128), F32), pltpu.SemaphoreType.DMA]
+        lines_out = jax.ShapeDtypeStruct((layers * shard_rows * PIECES, 128), F32)
+
         def scatter(layer, received, grads):
-            ins = [pl.BlockSpec((capacity * PIECES, 128), lambda i, *_: (i, 0))]
-            args = [to_lines(received)]
-            if grads is not None:
-                ins.append(ANY)
-                args.append(grads)
+            prior = [] if grads is None else [grads]
             return pl.pallas_call(
-                functools.partial(scatter_first if grads is None else scatter_next, layer),
-                out_shape=jax.ShapeDtypeStruct((layers * shard_rows * PIECES, 128), F32),
+                functools.partial(scatter_kernel, layer), out_shape=lines_out,
                 grid_spec=pltpu.PrefetchScalarGridSpec(
-                    num_scalar_prefetch=2, grid=(group_size,), in_specs=ins, out_specs=ANY,
-                    scratch_shapes=[pltpu.VMEM(((shard_rows + 8) * PIECES + PAD, 128), F32),
-                                    pltpu.VMEM((capacity * PIECES + PAD, 128), F32), pltpu.SemaphoreType.DMA]),
+                    num_scalar_prefetch=4, grid=(group_size,),
+                    in_specs=[half_spec, half_spec] + [ANY] * len(prior), out_specs=ANY, scratch_shapes=acc_scratch),
                 compiler_params=params(), name='scatter',
-                input_output_aliases={} if grads is None else {3: 0},
+                input_output_aliases={6: 0} if prior else {},
                 cost_estimate=cost(1e10, 4e7),
-            )(add_line, add_cnt, *args)
-
-        def gather(source, layer, line, src_rows, name):
+            )(add_line, n_base, n_over, at_over, to_lines(received[0]), to_lines(received[1]), *prior)
+
+        def scatter_rest(layer, received, grads):
+            return pl.pallas_call(
+                functools.partial(rest_kernel, layer), out_shape=lines_out,
+                grid_spec=pltpu.PrefetchScalarGridSpec(
+                    num_scalar_prefetch=2, grid=(group_size,),
+                    in_specs=[half_spec, ANY], out_specs=ANY, scratch_shapes=acc_scratch),
+                compiler_params=params(), name='scatter_rest', input_output_aliases={3: 0},
+                cost_estimate=cost(1e10, 4e7),
+            )(add_line, n_rest, to_lines(received), grads)
+
+        def send_home(a):
+            return exchange(a.reshape(group_size, half, d_emb)).reshape(slots // 2, d_emb)
+
+        def gather(source, layer, line, src_rows):
             n = source.shape[1]
             steps = n // src_rows
             return pl.pallas_call(
@@ -416,15 +472,15 @@
                     out_specs=pl.BlockSpec((TB, d_emb), lambda i, *_: (jnp.maximum(i - steps, 0), 0)),
                     scratch_shapes=[pltpu.VMEM((n * PIECES + PAD, 128), F32),
                                     pltpu.VMEM((TB * PIECES + PAD, 128), F32)]),
-                compiler_params=params(), name=name,
+                compiler_params=params(),
                 cost_estimate=cost(1e10, 2e7),
             )(line, source)
 
-        def tok_gather(a, rows, name):
-            return gather(a.reshape(1, n_tok, d_model), 0, line_of(rows), n_tok // 4, name)
+        def tok_gather(a, rows):
+            return gather(a.reshape(1, n_tok, d_model), 0, line_of(rows), n_tok // 4)
 
         def serve(layer, line):
-            return gather(tab_loc, layer, line, shard_rows // 3, 'serve').reshape(group_size, capacity, d_emb)
+            return gather(tab_loc, layer, line, shard_rows // 3).reshape(group_size, capacity, d_emb)
 
         def exchange(a):
             return lax.all_to_all(a, 'emb', 0, 0)
@@ -432,8 +488,8 @@
         served = serve(0, fetch_line)
         got = exchange(served)
         perm, served, later = lax.optimization_barrier((perm, served, fetch_line))
-        x = tok_gather(x_loc, perm, 'sort_x')
-        c = tok_gather(dy_loc, perm, 'sort_c')
+        x = tok_gather(x_loc, perm)
+        c = tok_gather(dy_loc, perm)
         served = serve(1, later)
         saved_x, saved_e, saved_g = [], [], []
         for layer in range(layers):
@@ -447,16 +503,19 @@
             x, e, g = forward(layer, x, here.reshape(slots, d_emb))
             saved_e.append(e)
             saved_g.append(g)
-        x_out = tok_gather(x, unperm, 'unsort')
+        x_out = tok_gather(x, unperm)
 
         grads = None
         pending = None
+        rests = []
         for layer in reversed(range(layers)):
             if layer == layers - 1:
-                s, send = rowgrad(layer, rowgrad_top_kernel, saved_x[layer], c, 1)
+                s, base, over, rest = rowgrad(layer, rowgrad_top_kernel, saved_x[layer], c, 1)
             else:
-                s, send = rowgrad(layer, rowgrad_kernel, saved_g[layer], c, 0)
-            got = lax.all_to_all(send.reshape(group_size, capacity, d_emb), 'emb', 0, 0).reshape(slots, d_emb)
+                s, base, over, rest = rowgrad(layer, rowgrad_kernel, saved_g[layer], c, 0)
+            rests.append((layer, rest))
+            base = send_home(base)
+            got = base, lax.all_gather(over, 'emb', axis=0, tiled=True)
             if pending is not None:
                 c, pending = lax.optimization_barrier((c, pending))
                 grads = scatter(layer + 1, pending, grads)
@@ -464,6 +523,15 @@
                 c = backward(layer, saved_x[layer], c, s, saved_e[layer])
             pending = got
         grads = scatter(0, pending, grads)
+
+        def add_rest(state):
+            left, acc = state
+            for layer, rest in rests:
+                rest, left = lax.optimization_barrier((rest, left))
+                acc = scatter_rest(layer, send_home(rest), acc)
+            return left - 1, acc
+
+        grads = lax.while_loop(lambda state: state[0] > 0, add_rest, (any_rest, grads))[1]
         return x_out, from_lines(grads, layers * shard_rows, d_emb).reshape(layers, shard_rows, d_emb)
 
     return jax.shard_map(body, mesh=mesh,

time: 1320 us -> 1310 us (level)
  waiting for transfers between devices: 129 us -> 91.6 us
  between operations: 16.3 us -> 30.2 us
    all_to_all x6 -> x1, waiting for transfers between devices: 104 us -> 4.78 us  [body(): lax.all_to_all(jnp.concatenate([send_ids, notes], axis=1), 'emb', 0, 0)]
    all_to_all x5 -> x10, waiting for transfers between devices: 24.2 us -> 86.6 us  [exchange(): return lax.all_to_all(a, 'emb', 0, 0)]
    all_to_all x5 -> x10, starting transfers between devices: 20.5 us -> 43.7 us  [exchange(): return lax.all_to_all(a, 'emb', 0, 0)]
    all_to_all x6 -> x1, starting transfers between devices: 26.6 us -> 4.27 us  [body(): lax.all_to_all(jnp.concatenate([send_ids, notes], axis=1), 'emb', 0, 0)]
  transfers between devices with their start and end apart: 11 -> 16, of which waited for: 6 -> 3; matrix products, arithmetic and copies ran while one was open for 1% -> 1% of each run, Pallas kernels for 79% -> 80%
where the time goes in v3:
time: 1310 us; the launch traced here: 1300 us
  Pallas kernels  1080 us (82%)
  waiting for transfers between devices  91.6 us (7%)
  starting transfers between devices  48.4 us (4%)
  other arithmetic  38.3 us (3%)
  between operations  30.2 us (2%)
    pallas_call x4, Pallas kernels, backward(): pl.pallas_call(bwd_kernel, out_shape=tok_out, grid=grid, in_specs=[tok_sp...  364 us
    pallas_call x5, Pallas kernels, forward(): pl.pallas_call(fwd_kernel, out_shape=[tok_out] * 3, grid_spec=pltpu.Prefe...  353 us
    pallas_call x5, Pallas kernels, scatter(): pl.pallas_call(functools.partial(scatter_kernel, layer), out_shape=lines_...  125 us
    pallas_call x8, Pallas kernels, gather(): pl.pallas_call(functools.partial(gather_kernel, steps), out_shape=jax.Sha...  123 us
    pallas_call x5, Pallas kernels, rowgrad(): pl.pallas_call(kernel, out_shape=[tok_out] + [jax.ShapeDtypeStruct((r, d_...  116 us
    all_to_all x10, waiting for transfers between devices, exchange(): return lax.all_to_all(a, 'emb', 0, 0)  86.6 us
    all_to_all x10, starting transfers between devices, exchange(): return lax.all_to_all(a, 'emb', 0, 0)  43.7 us
  transfers between devices with their start and end apart: 16, of which 3 were waited for; matrix products, arithmetic and copies ran while one was open for 1% of the time, Pallas kernels for 80%

profile of v3, /device:TPU:0, one launch (start us, length us, event | category | flops | bytes accessed | tf_op | source)
XLA Modules:
  0.0 1297.1 jit_solution(13179762352652555050)
XLA Ops:
  125.1 24.2 %all-to-all-done.6 = bf16[8,512,768]{2,1,0:T(8,128)(2,1)} async-done(((bf16[8,512,768]{2,1,0:T(8,128)(2,1)}), bf16[8,512,768]{2,1,0:T(8,128)(2,1)}, u32[]{:S(2)}, u32[]{:S(2)}) %all-to-all-start.6) | async-done | bytes 6291488 | tf_op jit(solution)/shard_map/all_to_all | solution.py:486
  159.5 15.8 %shard_map.108 = bf16[4096,768]{1,0:T(8,128)(2,1)} custom-call(s32[4096]{0:T(1024)} %fusion.11.line, bf16[5,6288,768]{2,1,0:T(8,128)(2,1)} %src_ref.9), custom_call_target="tpu_custom_call" | custom-call | flops 10000000000 | bytes 20000000 | tf_op jit(solution)/shard_map/pallas_call | solution.py:465
  175.4 70.7 %fwd.5 = (bf16[4096,768]{1,0:T(8,128)(2,1)}, bf16[4096,768]{1,0:T(8,128)(2,1)}, bf16[4096,768]{1,0:T(8,128)(2,1)}) custom-call(s32[16]{0:T(128)} %and_select_fusion.1.wst, s32[160]{0:T(256)} %get-tuple-element.262.chunk, bf16[4096,768]{1,0:T(8,128)(2,1)} %shard_map.105.x_ref, s32[4096,1]{1,0:T(8,128)} %add.296.posc_ref, bf16[5,768,3072]{2,1,0:T(8,128)(2,1)} %up_ref.17, ...), custom_call_target="tpu_custom_call" | custom-call | flops 48318382080 | bytes 30000000 | tf_op jit(solution)/shard_map/fwd/pallas_call | solution.py:398
  250.6 15.8 %shard_map.109 = bf16[4096,768]{1,0:T(8,128)(2,1)} custom-call(s32[4096]{0:T(1024)} %fusion.11.line, bf16[5,6288,768]{2,1,0:T(8,128)(2,1)} %src_ref.9), custom_call_target="tpu_custom_call" | custom-call | flops 10000000000 | bytes 20000000 | tf_op jit(solution)/shard_map/pallas_call | solution.py:465
  266.4 70.6 %fwd.6 = (bf16[4096,768]{1,0:T(8,128)(2,1)}, bf16[4096,768]{1,0:T(8,128)(2,1)}, bf16[4096,768]{1,0:T(8,128)(2,1)}) custom-call(s32[16]{0:T(128)} %and_select_fusion.1.wst, s32[160]{0:T(256)} %get-tuple-element.262.chunk, bf16[4096,768]{1,0:T(8,128)(2,1)} %get-tuple-element.202.x_ref, s32[4096,1]{1,0:T(8,128)} %add.296.posc_ref, ...), custom_call_target="tpu_custom_call" | custom-call | flops 48318382080 | bytes 30000000 | tf_op jit(solution)/shard_map/fwd/pallas_call | solution.py:398
  342.7 15.9 %shard_map.110 = bf16[4096,768]{1,0:T(8,128)(2,1)} custom-call(s32[4096]{0:T(1024)} %fusion.11.line, bf16[5,6288,768]{2,1,0:T(8,128)(2,1)} %src_ref.9), custom_call_target="tpu_custom_call" | custom-call | flops 10000000000 | bytes 20000000 | tf_op jit(solution)/shard_map/pallas_call | solution.py:465
  358.6 70.6 %fwd.7 = (bf16[4096,768]{1,0:T(8,128)(2,1)}, bf16[4096,768]{1,0:T(8,128)(2,1)}, bf16[4096,768]{1,0:T(8,128)(2,1)}) custom-call(s32[16]{0:T(128)} %and_select_fusion.1.wst, s32[160]{0:T(256)} %get-tuple-element.262.chunk, bf16[4096,768]{1,0:T(8,128)(2,1)} %get-tuple-element.208.x_ref, s32[4096,1]{1,0:T(8,128)} %add.296.posc_ref, ...), custom_call_target="tpu_custom_call" | custom-call | flops 48318382080 | bytes 30000000 | tf_op jit(solution)/shard_map/fwd/pallas_call | solution.py:398
  435.4 70.6 %fwd.8 = (bf16[4096,768]{1,0:T(8,128)(2,1)}, bf16[4096,768]{1,0:T(8,128)(2,1)}, bf16[4096,768]{1,0:T(8,128)(2,1)}) custom-call(s32[16]{0:T(128)} %and_select_fusion.1.wst, s32[160]{0:T(256)} %get-tuple-element.262.chunk, bf16[4096,768]{1,0:T(8,128)(2,1)} %get-tuple-element.214.x_ref, s32[4096,1]{1,0:T(8,128)} %add.296.posc_ref, ...), custom_call_target="tpu_custom_call" | custom-call | flops 48318382080 | bytes 30000000 | tf_op jit(solution)/shard_map/fwd/pallas_call | solution.py:398
  506.0 30.8 %rowgrad.5 = (bf16[4096,768]{1,0:T(8,128)(2,1)}, f32[2048,768]{1,0:T(8,128)}, f32[256,768]{1,0:T(8,128)}, f32[2048,768]{1,0:T(8,128)}) custom-call(s32[16]{0:T(128)} %and_select_fusion.1.wst, s32[160]{0:T(256)} %get-tuple-element.261.dest, s32[1]{0:T(128)} %bitcast.65.total, bf16[4096,768]{1,0:T(8,128)(2,1)} %get-tuple-element.216.x_ref, ...), custom_call_target="tpu_custom_call" | custom-call | flops 9663676416 | bytes 30000000 | tf_op jit(solution)/shard_map/rowgrad/pallas_call | solution.py:412
  536.9 70.9 %fwd.9 = (bf16[4096,768]{1,0:T(8,128)(2,1)}, bf16[4096,768]{1,0:T(8,128)(2,1)}, bf16[4096,768]{1,0:T(8,128)(2,1)}) custom-call(s32[16]{0:T(128)} %and_select_fusion.1.wst, s32[160]{0:T(256)} %get-tuple-element.262.chunk, bf16[4096,768]{1,0:T(8,128)(2,1)} %get-tuple-element.216.x_ref, s32[4096,1]{1,0:T(8,128)} %add.296.posc_ref, ...), custom_call_target="tpu_custom_call" | custom-call | flops 48318382080 | bytes 30000000 | tf_op jit(solution)/shard_map/fwd/pallas_call | solution.py:398
  614.8 90.7 %bwd.4.c_ref = bf16[4096,768]{1,0:T(8,128)(2,1)} custom-call(bf16[4096,768]{1,0:T(8,128)(2,1)} %get-tuple-element.216.x_ref, bf16[4096,768]{1,0:T(8,128)(2,1)} %shard_map.106.c_ref, bf16[4096,768]{1,0:T(8,128)(2,1)} %get-tuple-element.221.s_ref, bf16[4096,768]{1,0:T(8,128)(2,1)} %get-tuple-element.222.e_ref, bf16[5,768,3072]{2,1,0:T(8,128)(2,1)} %up_ref.17, ...), custom_call_target="tpu_custom_call" | custom-call | flops 67645734912 | bytes 40000000 | tf_op jit(solution)/shard_map/bwd/pallas_call | solution.py:424
  705.4 21.3 %rowgrad.6 = (bf16[4096,768]{1,0:T(8,128)(2,1)}, f32[2048,768]{1,0:T(8,128)}, f32[256,768]{1,0:T(8,128)}, f32[2048,768]{1,0:T(8,128)}) custom-call(s32[16]{0:T(128)} %and_select_fusion.1.wst, s32[160]{0:T(256)} %get-tuple-element.261.dest, s32[1]{0:T(128)} %bitcast.65.total, bf16[4096,768]{1,0:T(8,128)(2,1)} %get-tuple-element.226.g_ref, ...), custom_call_target="tpu_custom_call" | custom-call | flops 9663676416 | bytes 30000000 | tf_op jit(solution)/shard_map/rowgrad/pallas_call | solution.py:412
  730.4 91.2 %bwd.5.c_ref = bf16[4096,768]{1,0:T(8,128)(2,1)} custom-call(bf16[4096,768]{1,0:T(8,128)(2,1)} %get-tuple-element.214.x_ref, bf16[4096,768]{1,0:T(8,128)(2,1)} %bwd.4.c_ref, bf16[4096,768]{1,0:T(8,128)(2,1)} %get-tuple-element.227.s_ref, bf16[4096,768]{1,0:T(8,128)(2,1)} %get-tuple-element.228.e_ref, bf16[5,768,3072]{2,1,0:T(8,128)(2,1)} %up_ref.17, ...), custom_call_target="tpu_custom_call" | custom-call | flops 67645734912 | bytes 40000000 | tf_op jit(solution)/shard_map/bwd/pallas_call | solution.py:424
  821.6 21.3 %rowgrad.7 = (bf16[4096,768]{1,0:T(8,128)(2,1)}, f32[2048,768]{1,0:T(8,128)}, f32[256,768]{1,0:T(8,128)}, f32[2048,768]{1,0:T(8,128)}) custom-call(s32[16]{0:T(128)} %and_select_fusion.1.wst, s32[160]{0:T(256)} %get-tuple-element.261.dest, s32[1]{0:T(128)} %bitcast.65.total, bf16[4096,768]{1,0:T(8,128)(2,1)} %get-tuple-element.232.g_ref, ...), custom_call_target="tpu_custom_call" | custom-call | flops 9663676416 | bytes 30000000 | tf_op jit(solution)/shard_map/rowgrad/pallas_call | solution.py:412
  846.6 91.1 %bwd.6.c_ref = bf16[4096,768]{1,0:T(8,128)(2,1)} custom-call(bf16[4096,768]{1,0:T(8,128)(2,1)} %get-tuple-element.208.x_ref, bf16[4096,768]{1,0:T(8,128)(2,1)} %bwd.5.c_ref, bf16[4096,768]{1,0:T(8,128)(2,1)} %get-tuple-element.233.s_ref, bf16[4096,768]{1,0:T(8,128)(2,1)} %get-tuple-element.234.e_ref, bf16[5,768,3072]{2,1,0:T(8,128)(2,1)} %up_ref.17, ...), custom_call_target="tpu_custom_call" | custom-call | flops 67645734912 | bytes 40000000 | tf_op jit(solution)/shard_map/bwd/pallas_call | solution.py:424
  937.7 21.2 %rowgrad.8 = (bf16[4096,768]{1,0:T(8,128)(2,1)}, f32[2048,768]{1,0:T(8,128)}, f32[256,768]{1,0:T(8,128)}, f32[2048,768]{1,0:T(8,128)}) custom-call(s32[16]{0:T(128)} %and_select_fusion.1.wst, s32[160]{0:T(256)} %get-tuple-element.261.dest, s32[1]{0:T(128)} %bitcast.65.total, bf16[4096,768]{1,0:T(8,128)(2,1)} %get-tuple-element.238.g_ref, ...), custom_call_target="tpu_custom_call" | custom-call | flops 9663676416 | bytes 30000000 | tf_op jit(solution)/shard_map/rowgrad/pallas_call | solution.py:412
  959.0 90.9 %bwd.7.c_ref = bf16[4096,768]{1,0:T(8,128)(2,1)} custom-call(bf16[4096,768]{1,0:T(8,128)(2,1)} %get-tuple-element.202.x_ref, bf16[4096,768]{1,0:T(8,128)(2,1)} %bwd.6.c_ref, bf16[4096,768]{1,0:T(8,128)(2,1)} %get-tuple-element.239.s_ref, bf16[4096,768]{1,0:T(8,128)(2,1)} %get-tuple-element.240.e_ref, bf16[5,768,3072]{2,1,0:T(8,128)(2,1)} %up_ref.17, ...), custom_call_target="tpu_custom_call" | custom-call | flops 67645734912 | bytes 40000000 | tf_op jit(solution)/shard_map/bwd/pallas_call | solution.py:424
  1053.4 21.5 %rowgrad.9 = (bf16[4096,768]{1,0:T(8,128)(2,1)}, f32[2048,768]{1,0:T(8,128)}, f32[256,768]{1,0:T(8,128)}, f32[2048,768]{1,0:T(8,128)}) custom-call(s32[16]{0:T(128)} %and_select_fusion.1.wst, s32[160]{0:T(256)} %get-tuple-element.261.dest, s32[1]{0:T(128)} %bitcast.65.total, bf16[4096,768]{1,0:T(8,128)(2,1)} %get-tuple-element.219.g_ref, ...), custom_call_target="tpu_custom_call" | custom-call | flops 9663676416 | bytes 30000000 | tf_op jit(solution)/shard_map/rowgrad/pallas_call | solution.py:412
  1080.7 62.4 %all-to-all-done.15 = f32[8,256,768]{2,1,0:T(8,128)} async-done(((f32[8,256,768]{2,1,0:T(8,128)}), f32[8,256,768]{2,1,0:T(8,128)}, u32[]{:S(2)}, u32[]{:S(2)}) %all-to-all-start.15) | async-done | bytes 6291488 | tf_op jit(solution)/shard_map/all_to_all | solution.py:486
  1164.6 25.0 %scatter.5.refs_0_ = f32[188640,128]{1,0:T(8,128)} custom-call(s32[4096]{0:T(1024)S(1)} %fusion.15.line, s32[8]{0:T(128)} %get-tuple-element.314.n_base, s32[8]{0:T(128)} %get-tuple-element.313.n_over, s32[8]{0:T(128)} %get-tuple-element.312.at_over, f32[12288,128]{1,0:T(8,128)} %bitcast.104.base_ref, f32[12288,128]{1,0:T(8,128)} %bitcast.200), custom_call_target="tpu_custom_call" | custom-call | flops 10000000000 | bytes 40000000 | tf_op jit(solution)/shard_map/scatter/pallas_call | solution.py:439
  1189.6 25.0 %scatter.6.refs_0_ = f32[188640,128]{1,0:T(8,128)} custom-call(s32[4096]{0:T(1024)S(1)} %fusion.15.line, s32[8]{0:T(128)} %get-tuple-element.314.n_base, s32[8]{0:T(128)} %get-tuple-element.313.n_over, s32[8]{0:T(128)} %get-tuple-element.312.at_over, f32[12288,128]{1,0:T(8,128)} %bitcast.98.base_ref, ...), custom_call_target="tpu_custom_call", output_to_operand_aliasing={{}: (6, {})} | custom-call | flops 10000000000 | bytes 40000000 | tf_op jit(solution)/shard_map/scatter/pallas_call | solution.py:439
  1214.6 25.0 %scatter.7.refs_0_ = f32[188640,128]{1,0:T(8,128)} custom-call(s32[4096]{0:T(1024)S(1)} %fusion.15.line, s32[8]{0:T(128)} %get-tuple-element.314.n_base, s32[8]{0:T(128)} %get-tuple-element.313.n_over, s32[8]{0:T(128)} %get-tuple-element.312.at_over, f32[12288,128]{1,0:T(8,128)} %bitcast.92.base_ref, ...), custom_call_target="tpu_custom_call", output_to_operand_aliasing={{}: (6, {})} | custom-call | flops 10000000000 | bytes 40000000 | tf_op jit(solution)/shard_map/scatter/pallas_call | solution.py:439
  1239.7 25.0 %scatter.8.refs_0_ = f32[188640,128]{1,0:T(8,128)} custom-call(s32[4096]{0:T(1024)S(1)} %fusion.15.line, s32[8]{0:T(128)} %get-tuple-element.314.n_base, s32[8]{0:T(128)} %get-tuple-element.313.n_over, s32[8]{0:T(128)} %get-tuple-element.312.at_over, f32[12288,128]{1,0:T(8,128)} %bitcast.86.base_ref, ...), custom_call_target="tpu_custom_call", output_to_operand_aliasing={{}: (6, {})} | custom-call | flops 10000000000 | bytes 40000000 | tf_op jit(solution)/shard_map/scatter/pallas_call | solution.py:439
  1264.7 25.0 %scatter.9 = f32[188640,128]{1,0:T(8,128)} custom-call(s32[4096]{0:T(1024)S(1)} %fusion.15.line, s32[8]{0:T(128)} %get-tuple-element.314.n_base, s32[8]{0:T(128)} %get-tuple-element.313.n_over, s32[8]{0:T(128)} %get-tuple-element.312.at_over, f32[12288,128]{1,0:T(8,128)} %bitcast.78.base_ref, ...), custom_call_target="tpu_custom_call", output_to_operand_aliasing={{}: (6, {})} | custom-call | flops 10000000000 | bytes 40000000 | tf_op jit(solution)/shard_map/scatter/pallas_call | solution.py:439
  (126 shorter events, 174.4 us)
Async XLA Ops:
  47.5 9.0 all-to-all-start.5
  74.2 75.1 %all-to-all-start.6 = ((bf16[8,512,768]{2,1,0:T(8,128)(2,1)}), bf16[8,512,768]{2,1,0:T(8,128)(2,1)}, u32[]{:S(2)}, u32[]{:S(2)}) async-start(bf16[8,512,768]{2,1,0:T(8,128)(2,1)} %bitcast.196), calls=%async_computation.6 | async-start | bytes 12582912 | tf_op jit(solution)/shard_map/all_to_all | solution.py:486
  78.0 16.6 %copy-start = (s32[32,128]{1,0:T(8,128)}, s32[32,128]{1,0:T(8,128)S(1)}, u32[]{:S(2)}) copy-start(s32[32,128]{1,0:T(8,128)S(1)} %reduce-window.32) | copy-start | bytes 49156
  78.2 75.5 %copy-start.3 = (s32[4096]{0:T(1024)}, s32[4096]{0:T(1024)S(1)}, u32[]{:S(2)}) copy-start(s32[4096]{0:T(1024)S(1)} %select_reduce_fusion) | copy-start | bytes 49156
  78.5 16.0 %copy-start.6 = (s32[16,2,128]{2,1,0:T(2,128)}, s32[16,2,128]{2,1,0:T(2,128)S(1)}, u32[]{:S(2)}) copy-start(s32[16,2,128]{2,1,0:T(2,128)S(1)} %broadcast.446) | copy-start | bytes 49156
  149.3 96.8 %all-to-all-start.7 = ((bf16[8,512,768]{2,1,0:T(8,128)(2,1)}), bf16[8,512,768]{2,1,0:T(8,128)(2,1)}, u32[]{:S(2)}, u32[]{:S(2)}) async-start(bf16[8,512,768]{2,1,0:T(8,128)(2,1)} %bitcast.197), calls=%async_computation.7 | async-start | bytes 12582912 | tf_op jit(solution)/shard_map/all_to_all | solution.py:486
  246.0 91.0 %all-to-all-start.8 = ((bf16[8,512,768]{2,1,0:T(8,128)(2,1)}), bf16[8,512,768]{2,1,0:T(8,128)(2,1)}, u32[]{:S(2)}, u32[]{:S(2)}) async-start(bf16[8,512,768]{2,1,0:T(8,128)(2,1)} %bitcast.198), calls=%async_computation.8 | async-start | bytes 12582912 | tf_op jit(solution)/shard_map/all_to_all | solution.py:486
  337.1 92.1 %all-to-all-start.9 = ((bf16[8,512,768]{2,1,0:T(8,128)(2,1)}), bf16[8,512,768]{2,1,0:T(8,128)(2,1)}, u32[]{:S(2)}, u32[]{:S(2)}) async-start(bf16[8,512,768]{2,1,0:T(8,128)(2,1)} %bitcast.199), calls=%async_computation.9 | async-start | bytes 12582912 | tf_op jit(solution)/shard_map/all_to_all | solution.py:486
  429.2 5.6 copy-start.1
  429.2 5.6 copy-start.4
  429.2 107.7 %all-to-all-start.10 = ((bf16[8,512,768]{2,1,0:T(8,128)(2,1)}), bf16[8,512,768]{2,1,0:T(8,128)(2,1)}, u32[]{:S(2)}, u32[]{:S(2)}) async-start(bf16[8,512,768]{2,1,0:T(8,128)(2,1)} %bitcast.195), calls=%async_computation.10 | async-start | bytes 12582912 | tf_op jit(solution)/shard_map/all_to_all | solution.py:486
  434.6 292.3 %all-gather.6.cloned.1.call-start = ((), (), s32[]{:S(2)}) async-start(), calls=%async_computation.16 | async-start | bytes 7077888 | tf_op jit(solution)/shard_map/all_gather | solution.py:518
  607.8 119.0 %all-to-all-start.11 = ((f32[8,256,768]{2,1,0:T(8,128)}), f32[8,256,768]{2,1,0:T(8,128)}, u32[]{:S(2)}, u32[]{:S(2)}) async-start(f32[8,256,768]{2,1,0:T(8,128)} %bitcast.203), calls=%async_computation.11 | async-start | bytes 12582912 | tf_op jit(solution)/shard_map/all_to_all | solution.py:486
  614.7 228.3 %all-gather.8.cloned.1.call-start = ((), (), s32[]{:S(2)}) async-start(), calls=%async_computation.17 | async-start | bytes 7077888 | tf_op jit(solution)/shard_map/all_gather | solution.py:518
  726.8 116.2 %all-to-all-start.12 = ((f32[8,256,768]{2,1,0:T(8,128)}), f32[8,256,768]{2,1,0:T(8,128)}, u32[]{:S(2)}, u32[]{:S(2)}) async-start(f32[8,256,768]{2,1,0:T(8,128)} %bitcast.204), calls=%async_computation.12 | async-start | bytes 12582912 | tf_op jit(solution)/shard_map/all_to_all | solution.py:486
  730.4 228.6 %all-gather.10.cloned.1.call-start = ((), (), s32[]{:S(2)}) async-start(), calls=%async_computation.18 | async-start | bytes 7077888 | tf_op jit(solution)/shard_map/all_gather | solution.py:518
  843.0 115.9 %all-to-all-start.13 = ((f32[8,256,768]{2,1,0:T(8,128)}), f32[8,256,768]{2,1,0:T(8,128)}, u32[]{:S(2)}, u32[]{:S(2)}) async-start(f32[8,256,768]{2,1,0:T(8,128)} %bitcast.205), calls=%async_computation.13 | async-start | bytes 12582912 | tf_op jit(solution)/shard_map/all_to_all | solution.py:486
  846.5 393.1 %all-gather.14.cloned.1.call-start = ((), (), s32[]{:S(2)}) async-start(), calls=%async_computation.20 | async-start | bytes 7077888 | tf_op jit(solution)/shard_map/all_gather | solution.py:518
  1049.8 93.3 %all-to-all-start.15 = ((f32[8,256,768]{2,1,0:T(8,128)}), f32[8,256,768]{2,1,0:T(8,128)}, u32[]{:S(2)}, u32[]{:S(2)}) async-start(f32[8,256,768]{2,1,0:T(8,128)} %bitcast.202), calls=%async_computation.15 | async-start | bytes 12582912 | tf_op jit(solution)/shard_map/all_to_all | solution.py:486
  1053.3 211.4 %all-gather.12.cloned.1.call-start = ((), (), s32[]{:S(2)}) async-start(), calls=%async_computation.19 | async-start | bytes 7077888 | tf_op jit(solution)/shard_map/all_gather | solution.py:518
  1053.4 21.6 %copy-start.8 = (s32[4096]{0:T(1024)S(1)}, s32[4096]{0:T(1024)}, u32[]{:S(2)}) copy-start(s32[4096]{0:T(1024)} %get-tuple-element.295) | copy-start | bytes 49156
  1143.1 5.8 copy-start.10
  1143.1 121.6 %all-to-all-start.14 = ((f32[8,256,768]{2,1,0:T(8,128)}), f32[8,256,768]{2,1,0:T(8,128)}, u32[]{:S(2)}, u32[]{:S(2)}) async-start(f32[8,256,768]{2,1,0:T(8,128)} %bitcast.201), calls=%async_computation.14 | async-start | bytes 12582912 | tf_op jit(solution)/shard_map/all_to_all | solution.py:486
  1264.7 25.0 %copy-start.2 = (s32[8]{0:T(128)S(1)}, s32[8]{0:T(128)}, u32[]{:S(2)}) copy-start(s32[8]{0:T(128)} %get-tuple-element.420) | copy-start | bytes 100
  (3 other events, 10.5 us)
Sparse Core Ops, SparseCore 0:
  537.0 42.9 all-gather.5
  726.9 84.1 all-gather.7
  843.1 84.1 all-gather.9
  959.1 40.8 all-gather.13
  1075.0 76.9 all-gather.11

commit v4 on v3

--- a/solution.py
+++ b/solution.py
@@ -92,14 +92,10 @@
 def rowgrad_top_kernel(wst, dest, total, x_ref, c_ref, posr_ref, gt_ref, pj_ref, *refs):
     u = norm_rows(x_ref[...].astype(F32))[0].astype(BF16)
     g = gelu(dot(u, gt_ref[0])).astype(BF16)
-    rowgrad_body(wst, dest, total, g, c_ref, posr_ref, pj_ref, *refs)
-
-
-def rowgrad_kernel(wst, dest, total, g_ref, c_ref, posr_ref, pj_ref, *refs):
-    rowgrad_body(wst, dest, total, g_ref[...], c_ref, posr_ref, pj_ref, *refs)
-
-
-def rowgrad_body(wst, dest, total, g, c_ref, posr_ref, pj_ref, s_ref, base_ref, over_ref, rest_ref, acc, sem):
+    rowgrad_body(wst, dest, total, g, c_ref[...], posr_ref, pj_ref, *refs)
+
+
+def rowgrad_body(wst, dest, total, g, c, posr_ref, pj_ref, s_ref, base_ref, over_ref, rest_ref, acc, sem):
     i = pl.program_id(0)
     last = pl.num_programs(0) - 1
 
@@ -107,8 +103,8 @@
     def _():
         acc[...] = jnp.zeros_like(acc)
 
-    tb = c_ref.shape[0]
-    s = dot_nt(c_ref[...], pj_ref[0]).astype(BF16)
+    tb = c.shape[0]
+    s = dot_nt(c, pj_ref[0]).astype(BF16)
     s_ref[...] = s
     k = g.astype(F32) * s.astype(F32)
     hi = k.astype(BF16)
@@ -144,7 +140,8 @@
         lax.fori_loop(0, total[0], wait, 0)
 
 
-def bwd_kernel(x_ref, c_ref, s_ref, e_ref, up_ref, dn_ref, gt_ref, co_ref):
+def bwd_kernel(wst, dest, total, x_ref, c_ref, s_ref, e_ref, up_ref, dn_ref, gt_ref, g_ref, posr_ref, pj_ref,
+               co_ref, *refs):
     xf = x_ref[...].astype(F32)
     n, inv = norm_rows(xf)
     u = n.astype(BF16)
@@ -160,7 +157,9 @@
         da = (gelu_grad(a) * dh.astype(F32)).astype(BF16)
         du = du + dot_nt(da, w_k)
     dx = inv * (du - n * jnp.mean(du * n, axis=-1, keepdims=True))
-    co_ref[...] = (c.astype(F32) + dx).astype(BF16)
+    down = (c.astype(F32) + dx).astype(BF16)
+    co_ref[...] = down
+    rowgrad_body(wst, dest, total, g_ref[...], down, posr_ref, pj_ref, *refs)
 
 
 def line_of(row):
@@ -213,25 +212,37 @@
         lax.fori_loop(0, out_rows // CH, narrow, 0, unroll=2)
 
 
-def add_rows(line, at, groups, recv_ref, first, acc, stage):
+def add_rows(line, at, groups, recv_ref, first, acc, offset, stage):
     span = 8 * PIECES
-
-    def load(t, carry):
-        src = pl.ds(pl.multiple_of(first + t * span, 8), span)
-        stage[pl.ds(pl.multiple_of(t * span, 8), span), :] = recv_ref[src, :]
-        return carry
-
-    def group(t, carry):
-        base = pl.multiple_of(t * span, 8)
-        to = [line[at + t * 8 + q] for q in range(8)]
-        old = [acc[piece_rows(r), :] for r in to]
-        new = [o + stage[piece_rows(base + q), :] for q, o in enumerate(old)]
+    inside = jnp.maximum((recv_ref.shape[0] - first) // span - 1, 0)
+
+    def add(t, read):
+        to = [line[at + t * 8 + q] + offset for q in range(8)]
+        new = [acc[piece_rows(r), :] + read(q) for q, r in enumerate(to)]
         for r, v in zip(to, new):
             acc[piece_rows(r), :] = v
+
+    def group(t, carry):
+        base = pl.multiple_of(first + t * span, 8)
+        add(t, lambda q: recv_ref[piece_rows(base + q), :])
         return carry
 
-    lax.fori_loop(0, groups, load, 0)
-    lax.fori_loop(0, groups, group, 0)
+    lax.fori_loop(0, jnp.minimum(groups, inside), group, 0)
+
+    @pl.when(groups > inside)
+    def _():
+        stage[0:span, :] = recv_ref[recv_ref.shape[0] - span:, :]
+        add(inside, lambda q: stage[piece_rows(q), :])
+
+
+def clear_lines(acc, first, size):
+    span = 8 * PIECES
+
+    def clear(t, carry):
+        acc[pl.ds(pl.multiple_of(first + t * span, 8), span), :] = jnp.zeros((span, 128), F32)
+        return carry
+
+    lax.fori_loop(0, size // span, clear, 0, unroll=2)
 
 
 def store_layer(layer, out_ref, acc, sem, back=False):
@@ -242,26 +253,58 @@
     cp.wait()
 
 
-def scatter_kernel(layer, line, n_base, n_over, at_over, base_ref, over_ref, *refs):
-    out_ref, acc, stage, sem = refs[-4:]
+def scatter_kernel(layer, line, n_base, n_over, at_over, base_ref, over_ref, _, out_ref, acc, stage, sem):
     i = pl.program_id(0)
-    span = 8 * PIECES
-    cap = base_ref.shape[0] // PIECES + over_ref.shape[0] // PIECES
+    half = base_ref.shape[0] // PIECES
 
     @pl.when(i == 0)
     def _():
-        def clear(t, carry):
-            acc[pl.ds(pl.multiple_of(t * span, 8), span), :] = jnp.zeros((span, 128), F32)
-            return carry
-
-        lax.fori_loop(0, (acc.shape[0] - PAD) // span, clear, 0, unroll=2)
-
-    add_rows(line, i * cap, (n_base[i] + 7) // 8, base_ref, 0, acc, stage)
-    add_rows(line, i * cap + cap // 2, (n_over[i] + 7) // 8, over_ref, at_over[i] * (CH * PIECES), acc, stage)
+        clear_lines(acc, 0, acc.shape[0] - PAD)
+
+    add_rows(line, 2 * i * half, (n_base[i] + 7) // 8, base_ref, 0, acc, 0, stage)
+    add_rows(line, (2 * i + 1) * half, (n_over[i] + 7) // 8, over_ref, at_over[i] * (CH * PIECES), acc, 0, stage)
 
     @pl.when(i == pl.num_programs(0) - 1)
     def _():
         store_layer(layer, out_ref, acc, sem)
+
+
+def scatter_many_kernel(order, line, n_base, n_over, at_over, *refs):
+    n = len(order)
+    recv, (out_ref, acc, stage, sem) = refs[:2 * n], refs[2 * n:]
+    p, i = pl.program_id(0), pl.program_id(1)
+    last = pl.num_programs(1) - 1
+    half = recv[0].shape[0] // PIECES
+    slot_lines = (acc.shape[0] - PAD) // 2
+    size = slot_lines - 8 * PIECES
+    offset = lax.rem(p, 2) * slot_lines
+
+    def store(at):
+        slot = at % 2
+        return pltpu.make_async_copy(acc.at[pl.ds(slot * slot_lines, size)],
+                                     out_ref.at[pl.ds(order[at] * size, size)], sem.at[slot])
+
+    for at in range(n):
+        @pl.when(p == at)
+        def _():
+            @pl.when(i == 0)
+            def _():
+                if at >= 2:
+                    store(at - 2).wait()
+                clear_lines(acc, (at % 2) * slot_lines, slot_lines)
+
+            base_ref, over_ref = recv[2 * at], recv[2 * at + 1]
+            add_rows(line, 2 * i * half, (n_base[i] + 7) // 8, base_ref, 0, acc, offset, stage)
+            add_rows(line, (2 * i + 1) * half, (n_over[i] + 7) // 8, over_ref, at_over[i] * (CH * PIECES), acc, offset,
+                     stage)
+
+            @pl.when(i == last)
+            def _():
+                store(at).start()
+                if at == n - 1:
+                    if n > 1:
+                        store(at - 1).wait()
+                    store(at).wait()
 
 
 def rest_kernel(layer, line, n_rest, rest_ref, _, out_ref, acc, stage, sem):
@@ -272,7 +315,7 @@
     def _():
         store_layer(layer, out_ref, acc, sem, back=True)
 
-    add_rows(line, i * cap + cap // 2, (n_rest[i] + 7) // 8, rest_ref, 0, acc, stage)
+    add_rows(line, i * cap + cap // 2, (n_rest[i] + 7) // 8, rest_ref, 0, acc, 0, stage)
 
     @pl.when(i == pl.num_programs(0) - 1)
     def _():
@@ -328,7 +371,6 @@
         order = lax.sort(tok_id * n_tok + iota)
         perm = order % n_tok
         sid = order // n_tok
-        unperm = lax.sort(perm * n_tok + iota) % n_tok
         is_new = jnp.concatenate([jnp.ones((1,), jnp.bool_), sid[1:] != sid[:-1]])
         rank = jnp.cumsum(is_new.astype(I32)) - 1
         used = lax.sort(jnp.where(is_new, sid, jnp.int32(2 ** 30)))[:n_uniq]
@@ -407,44 +449,64 @@
                 cost_estimate=cost(2 * mm + 2 * sq, 3e7),
             )(wst, chunk, x, posc, w_up, w_down, w_gate, w_proj, returned)
 
-        def rowgrad(layer, kernel, operand, c, gate):
-            weights = [w_gate] * gate + [w_proj]
-            return pl.pallas_call(
-                kernel, out_shape=[tok_out] + [jax.ShapeDtypeStruct((r, d_emb), F32) for r in (slots // 2, half, slots // 2)],
+        send_out = [jax.ShapeDtypeStruct((r, d_emb), F32) for r in (slots // 2, half, slots // 2)]
+        row_scratch = [pltpu.VMEM((n_rows, d_emb), F32), pltpu.SemaphoreType.DMA]
+
+        def rowgrad_top(layer, x, c):
+            return pl.pallas_call(
+                rowgrad_top_kernel, out_shape=[tok_out, *send_out],
                 grid_spec=pltpu.PrefetchScalarGridSpec(
                     num_scalar_prefetch=3, grid=grid,
-                    in_specs=[tok_spec, tok_spec, posr_spec, *w_specs(layer, *[s_sq] * len(weights))],
-                    out_specs=[tok_spec, ANY, ANY, ANY],
-                    scratch_shapes=[pltpu.VMEM((n_rows, d_emb), F32), pltpu.SemaphoreType.DMA]),
+                    in_specs=[tok_spec, tok_spec, posr_spec, *w_specs(layer, s_sq, s_sq)],
+                    out_specs=[tok_spec, ANY, ANY, ANY], scratch_shapes=row_scratch),
                 compiler_params=params(), name='rowgrad',
                 cost_estimate=cost(2 * sq, 3e7),
-            )(wst, dest, total, operand, c, posr, *weights)
-
-        def backward(layer, x, c, s, e):
-            return pl.pallas_call(
-                bwd_kernel, out_shape=tok_out, grid=grid,
-                in_specs=[tok_spec] * 4 + w_specs(layer, s_up, s_dn, s_sq),
-                out_specs=tok_spec,
+            )(wst, dest, total, x, c, posr, w_gate, w_proj)
+
+        def backward(layer, x, c, s, e, g_below):
+            return pl.pallas_call(
+                bwd_kernel, out_shape=[tok_out, tok_out, *send_out],
+                grid_spec=pltpu.PrefetchScalarGridSpec(
+                    num_scalar_prefetch=3, grid=grid,
+                    in_specs=[tok_spec] * 4 + w_specs(layer, s_up, s_dn, s_sq)
+                    + [tok_spec, posr_spec] + w_specs(layer - 1, s_sq),
+                    out_specs=[tok_spec, tok_spec, ANY, ANY, ANY], scratch_shapes=row_scratch),
                 compiler_params=params(), name='bwd',
-                cost_estimate=cost(3 * mm + 2 * sq, 4e7),
-            )(x, c, s, e, w_up, w_down, w_gate)
+                cost_estimate=cost(3 * mm + 4 * sq, 6e7),
+            )(wst, dest, total, x, c, s, e, w_up, w_down, w_gate, g_below, posr, w_proj)
 
         half_spec = pl.BlockSpec((half * PIECES, 128), lambda i, *_: (i, 0))
         acc_scratch = [pltpu.VMEM(((shard_rows + 8) * PIECES + PAD, 128), F32),
-                       pltpu.VMEM((half * PIECES + PAD, 128), F32), pltpu.SemaphoreType.DMA]
+                       pltpu.VMEM((8 * PIECES + PAD, 128), F32), pltpu.SemaphoreType.DMA]
         lines_out = jax.ShapeDtypeStruct((layers * shard_rows * PIECES, 128), F32)
 
         def scatter(layer, received, grads):
-            prior = [] if grads is None else [grads]
             return pl.pallas_call(
                 functools.partial(scatter_kernel, layer), out_shape=lines_out,
                 grid_spec=pltpu.PrefetchScalarGridSpec(
                     num_scalar_prefetch=4, grid=(group_size,),
-                    in_specs=[half_spec, half_spec] + [ANY] * len(prior), out_specs=ANY, scratch_shapes=acc_scratch),
-                compiler_params=params(), name='scatter',
-                input_output_aliases={6: 0} if prior else {},
+                    in_specs=[half_spec, half_spec, ANY], out_specs=ANY, scratch_shapes=acc_scratch),
+                compiler_params=params(), name='scatter', input_output_aliases={6: 0},
                 cost_estimate=cost(1e10, 4e7),
-            )(add_line, n_base, n_over, at_over, to_lines(received[0]), to_lines(received[1]), *prior)
+            )(add_line, n_base, n_over, at_over, to_lines(received[0]), to_lines(received[1]), grads)
+
+        def scatter_many(order, received):
+            def at_layer(at):
+                return pl.BlockSpec(
+                    (half * PIECES, 128),
+                    lambda p, i, *_: (jnp.where(p == at, i, jnp.where(p < at, 0, group_size - 1)), 0))
+
+            return pl.pallas_call(
+                functools.partial(scatter_many_kernel, order), out_shape=lines_out,
+                grid_spec=pltpu.PrefetchScalarGridSpec(
+                    num_scalar_prefetch=4, grid=(len(order), group_size),
+                    in_specs=[at_layer(at) for at in range(len(order)) for _ in range(2)], out_specs=ANY,
+                    scratch_shapes=[pltpu.VMEM((2 * (shard_rows + 8) * PIECES + PAD, 128), F32),
+                                    pltpu.VMEM((8 * PIECES + PAD, 128), F32), pltpu.SemaphoreType.DMA((2,))]),
+                compiler_params=pltpu.CompilerParams(dimension_semantics=('arbitrary', 'arbitrary'),
+                                                     vmem_limit_bytes=VMEM_LIMIT),
+                name='scatter_many', cost_estimate=cost(4e10, 1.6e8),
+            )(add_line, n_base, n_over, at_over, *[to_lines(a) for pair in received for a in pair])
 
         def scatter_rest(layer, received, grads):
             return pl.pallas_call(
@@ -487,42 +549,38 @@
 
         served = serve(0, fetch_line)
         got = exchange(served)
-        perm, served, later = lax.optimization_barrier((perm, served, fetch_line))
+        perm, unperm, served, later = lax.optimization_barrier((perm, perm * n_tok + iota, served, fetch_line))
+        unperm = lax.sort(unperm) % n_tok
         x = tok_gather(x_loc, perm)
         c = tok_gather(dy_loc, perm)
-        served = serve(1, later)
+        ready = [serve(layer, later) for layer in range(1, min(3, layers))]
         saved_x, saved_e, saved_g = [], [], []
         for layer in range(layers):
             here = got
             if layer + 1 < layers:
-                x, c, here, served, later = lax.optimization_barrier((x, c, here, served, later))
-                got = exchange(served)
-                if layer + 2 < layers:
-                    served = serve(layer + 2, later)
+                x, c, unperm, here, ready, later = lax.optimization_barrier((x, c, unperm, here, ready, later))
+                got = exchange(ready.pop(0))
+                if layer + 3 < layers:
+                    ready.append(serve(layer + 3, later))
             saved_x.append(x)
             x, e, g = forward(layer, x, here.reshape(slots, d_emb))
             saved_e.append(e)
             saved_g.append(g)
         x_out = tok_gather(x, unperm)
 
-        grads = None
-        pending = None
         rests = []
+        homes = []
+        s, base, over, rest = rowgrad_top(layers - 1, saved_x[layers - 1], c)
         for layer in reversed(range(layers)):
-            if layer == layers - 1:
-                s, base, over, rest = rowgrad(layer, rowgrad_top_kernel, saved_x[layer], c, 1)
-            else:
-                s, base, over, rest = rowgrad(layer, rowgrad_kernel, saved_g[layer], c, 0)
             rests.append((layer, rest))
             base = send_home(base)
-            got = base, lax.all_gather(over, 'emb', axis=0, tiled=True)
-            if pending is not None:
-                c, pending = lax.optimization_barrier((c, pending))
-                grads = scatter(layer + 1, pending, grads)
+            homes.append((base, lax.all_gather(over, 'emb', axis=0, tiled=True)))
             if layer > 0:
-                c = backward(layer, saved_x[layer], c, s, saved_e[layer])
-            pending = got
-        grads = scatter(0, pending, grads)
+                if len(homes) > 1:
+                    c, homes[-2] = lax.optimization_barrier((c, homes[-2]))
+                c, s, base, over, rest = backward(layer, saved_x[layer], c, s, saved_e[layer], saved_g[layer - 1])
+        grads = scatter_many(tuple(range(layers - 1, 0, -1)), homes[:-1])
+        grads = scatter(0, homes[-1], grads)
 
         def add_rest(state):
             left, acc = state

time: 1310 us -> 1210 us (0.924)
  waiting for transfers between devices: 91.6 us -> 17.3 us
  Pallas kernels: 1080 us -> 1050 us
    pallas_call x5 -> x1, Pallas kernels: 125 us -> 21.9 us  [scatter(): pl.pallas_call(functools.partial(scatter_kernel, layer), out_shape=lines_...]
    all_to_all x10, waiting for transfers between devices: 86.6 us -> 12.4 us  [exchange(): return lax.all_to_all(a, 'emb', 0, 0)]
    pallas_call x9 -> x6, Pallas kernels: 480 us -> 547 us  [the longest x4 445 us: backward(): pl.pallas_call(bwd_kernel, out_shape=[tok_out, tok_out, *send_out], grid_...]
  transfers between devices with their start and end apart: 16 -> 16, of which waited for: 3 -> 4; matrix products, arithmetic and copies ran while one was open for 1% -> 2% of each run, Pallas kernels for 80% -> 85%
where the time goes in v4:
time: 1210 us; the launch traced here: 1200 us
  Pallas kernels  1050 us (87%)
  starting transfers between devices  54.3 us (4%)
  other arithmetic  37.8 us (3%)
  between operations  30.2 us (2%)
  waiting for transfers between devices  17.3 us (1%)
    pallas_call x4, Pallas kernels, backward(): pl.pallas_call(bwd_kernel, out_shape=[tok_out, tok_out, *send_out], grid_...  445 us
    pallas_call x5, Pallas kernels, forward(): pl.pallas_call(fwd_kernel, out_shape=[tok_out] * 3, grid_spec=pltpu.Prefe...  357 us
    pallas_call x8, Pallas kernels, gather(): pl.pallas_call(functools.partial(gather_kernel, steps), out_shape=jax.Sha...  123 us
    pallas_call x1, Pallas kernels, scatter_many(): pl.pallas_call(functools.partial(scatter_many_kernel, order), out_shape=l...  71.5 us
    all_to_all x10, starting transfers between devices, exchange(): return lax.all_to_all(a, 'emb', 0, 0)  49.5 us
    pallas_call x1, Pallas kernels, rowgrad_top(): pl.pallas_call(rowgrad_top_kernel, out_shape=[tok_out, *send_out], grid_s...  31.4 us
  transfers between devices with their start and end apart: 16, of which 4 were waited for; matrix products, arithmetic and copies ran while one was open for 2% of the time, Pallas kernels for 85%

profile of v4, /device:TPU:0, one launch (start us, length us, event | category | flops | bytes accessed | tf_op | source)
XLA Modules:
  0.0 1195.9 jit_solution(7334436310685025164)
XLA Ops:
  58.0 15.8 %shard_map.104 = bf16[4096,768]{1,0:T(8,128)(2,1)} custom-call(s32[4096]{0:T(1024)} %fusion.8.line, bf16[5,6288,768]{2,1,0:T(8,128)(2,1)} %src_ref.9), custom_call_target="tpu_custom_call" | custom-call | flops 10000000000 | bytes 20000000 | tf_op jit(solution)/shard_map/pallas_call | solution.py:527
  86.0 15.9 %shard_map.107 = bf16[4096,768]{1,0:T(8,128)(2,1)} custom-call(s32[4096]{0:T(1024)} %fusion.8.line, bf16[5,6288,768]{2,1,0:T(8,128)(2,1)} %src_ref.9), custom_call_target="tpu_custom_call" | custom-call | flops 10000000000 | bytes 20000000 | tf_op jit(solution)/shard_map/pallas_call | solution.py:527
  101.8 15.8 %shard_map.108 = bf16[4096,768]{1,0:T(8,128)(2,1)} custom-call(s32[4096]{0:T(1024)} %fusion.8.line, bf16[5,6288,768]{2,1,0:T(8,128)(2,1)} %src_ref.9), custom_call_target="tpu_custom_call" | custom-call | flops 10000000000 | bytes 20000000 | tf_op jit(solution)/shard_map/pallas_call | solution.py:527
  117.7 14.6 %shard_map.105.x_ref = bf16[4096,768]{1,0:T(8,128)(2,1)} custom-call(s32[4096]{0:T(1024)} %fusion.10.line, bf16[1,4096,768]{2,1,0:T(8,128)(2,1)} %bitcast.227), custom_call_target="tpu_custom_call" | custom-call | flops 10000000000 | bytes 20000000 | tf_op jit(solution)/shard_map/pallas_call | solution.py:527
  132.3 14.6 %shard_map.106.c_ref = bf16[4096,768]{1,0:T(8,128)(2,1)} custom-call(s32[4096]{0:T(1024)} %fusion.10.line, bf16[1,4096,768]{2,1,0:T(8,128)(2,1)} %bitcast.228), custom_call_target="tpu_custom_call" | custom-call | flops 10000000000 | bytes 20000000 | tf_op jit(solution)/shard_map/pallas_call | solution.py:527
  159.2 15.9 %shard_map.109 = bf16[4096,768]{1,0:T(8,128)(2,1)} custom-call(s32[4096]{0:T(1024)} %fusion.8.line, bf16[5,6288,768]{2,1,0:T(8,128)(2,1)} %src_ref.9), custom_call_target="tpu_custom_call" | custom-call | flops 10000000000 | bytes 20000000 | tf_op jit(solution)/shard_map/pallas_call | solution.py:527
  175.1 71.6 %fwd.5 = (bf16[4096,768]{1,0:T(8,128)(2,1)}, bf16[4096,768]{1,0:T(8,128)(2,1)}, bf16[4096,768]{1,0:T(8,128)(2,1)}) custom-call(s32[16]{0:T(128)} %and_select_fusion.1.wst, s32[160]{0:T(256)} %get-tuple-element.278.chunk, bf16[4096,768]{1,0:T(8,128)(2,1)} %shard_map.105.x_ref, s32[4096,1]{1,0:T(8,128)} %add.294.posc_ref, bf16[5,768,3072]{2,1,0:T(8,128)(2,1)} %up_ref.17, ...), custom_call_target="tpu_custom_call" | custom-call | flops 48318382080 | bytes 30000000 | tf_op jit(solution)/shard_map/fwd/pallas_call | solution.py:440
  246.8 6.4 all-to-all-start.8
  253.2 15.9 %shard_map.110 = bf16[4096,768]{1,0:T(8,128)(2,1)} custom-call(s32[4096]{0:T(1024)} %fusion.8.line, bf16[5,6288,768]{2,1,0:T(8,128)(2,1)} %src_ref.9), custom_call_target="tpu_custom_call" | custom-call | flops 10000000000 | bytes 20000000 | tf_op jit(solution)/shard_map/pallas_call | solution.py:527
  269.0 71.6 %fwd.6 = (bf16[4096,768]{1,0:T(8,128)(2,1)}, bf16[4096,768]{1,0:T(8,128)(2,1)}, bf16[4096,768]{1,0:T(8,128)(2,1)}) custom-call(s32[16]{0:T(128)} %and_select_fusion.1.wst, s32[160]{0:T(256)} %get-tuple-element.278.chunk, bf16[4096,768]{1,0:T(8,128)(2,1)} %get-tuple-element.213.x_ref, s32[4096,1]{1,0:T(8,128)} %add.294.posc_ref, ...), custom_call_target="tpu_custom_call" | custom-call | flops 48318382080 | bytes 30000000 | tf_op jit(solution)/shard_map/fwd/pallas_call | solution.py:440
  340.6 7.9 all-to-all-start.9
  348.5 70.7 %fwd.7 = (bf16[4096,768]{1,0:T(8,128)(2,1)}, bf16[4096,768]{1,0:T(8,128)(2,1)}, bf16[4096,768]{1,0:T(8,128)(2,1)}) custom-call(s32[16]{0:T(128)} %and_select_fusion.1.wst, s32[160]{0:T(256)} %get-tuple-element.278.chunk, bf16[4096,768]{1,0:T(8,128)(2,1)} %get-tuple-element.221.x_ref, s32[4096,1]{1,0:T(8,128)} %add.294.posc_ref, ...), custom_call_target="tpu_custom_call" | custom-call | flops 48318382080 | bytes 30000000 | tf_op jit(solution)/shard_map/fwd/pallas_call | solution.py:440
  425.5 70.7 %fwd.8 = (bf16[4096,768]{1,0:T(8,128)(2,1)}, bf16[4096,768]{1,0:T(8,128)(2,1)}, bf16[4096,768]{1,0:T(8,128)(2,1)}) custom-call(s32[16]{0:T(128)} %and_select_fusion.1.wst, s32[160]{0:T(256)} %get-tuple-element.278.chunk, bf16[4096,768]{1,0:T(8,128)(2,1)} %get-tuple-element.229.x_ref, s32[4096,1]{1,0:T(8,128)} %add.294.posc_ref, ...), custom_call_target="tpu_custom_call" | custom-call | flops 48318382080 | bytes 30000000 | tf_op jit(solution)/shard_map/fwd/pallas_call | solution.py:440
  496.2 31.4 %rowgrad.1 = (bf16[4096,768]{1,0:T(8,128)(2,1)}, f32[2048,768]{1,0:T(8,128)}, f32[256,768]{1,0:T(8,128)}, f32[2048,768]{1,0:T(8,128)}) custom-call(s32[16]{0:T(128)} %and_select_fusion.1.wst, s32[160]{0:T(256)} %get-tuple-element.277.dest, s32[1]{0:T(128)} %bitcast.65.total, bf16[4096,768]{1,0:T(8,128)(2,1)} %get-tuple-element.231.x_ref, ...), custom_call_target="tpu_custom_call" | custom-call | flops 9663676416 | bytes 30000000 | tf_op jit(solution)/shard_map/rowgrad/pallas_call | solution.py:456
  527.6 72.0 %fwd.9 = (bf16[4096,768]{1,0:T(8,128)(2,1)}, bf16[4096,768]{1,0:T(8,128)(2,1)}, bf16[4096,768]{1,0:T(8,128)(2,1)}) custom-call(s32[16]{0:T(128)} %and_select_fusion.1.wst, s32[160]{0:T(256)} %get-tuple-element.278.chunk, bf16[4096,768]{1,0:T(8,128)(2,1)} %get-tuple-element.231.x_ref, s32[4096,1]{1,0:T(8,128)} %add.294.posc_ref, ...), custom_call_target="tpu_custom_call" | custom-call | flops 48318382080 | bytes 30000000 | tf_op jit(solution)/shard_map/fwd/pallas_call | solution.py:440
  599.6 9.2 all-to-all-start.11
  608.9 110.7 %bwd.4 = (bf16[4096,768]{1,0:T(8,128)(2,1)}, bf16[4096,768]{1,0:T(8,128)(2,1)}, f32[2048,768]{1,0:T(8,128)}, f32[256,768]{1,0:T(8,128)}, f32[2048,768]{1,0:T(8,128)}) custom-call(s32[16]{0:T(128)} %and_select_fusion.1.wst, s32[160]{0:T(256)} %get-tuple-element.277.dest, s32[1]{0:T(128)} %bitcast.65.total, bf16[4096,768]{1,0:T(8,128)(2,1)} %get-tuple-element.231.x_ref, ...), custom_call_target="tpu_custom_call" | custom-call | flops 77309411328 | bytes 60000000 | tf_op jit(solution)/shard_map/bwd/pallas_call | solution.py:467
  723.3 111.3 %bwd.5 = (bf16[4096,768]{1,0:T(8,128)(2,1)}, bf16[4096,768]{1,0:T(8,128)(2,1)}, f32[2048,768]{1,0:T(8,128)}, f32[256,768]{1,0:T(8,128)}, f32[2048,768]{1,0:T(8,128)}) custom-call(s32[16]{0:T(128)} %and_select_fusion.1.wst, s32[160]{0:T(256)} %get-tuple-element.277.dest, s32[1]{0:T(128)} %bitcast.65.total, bf16[4096,768]{1,0:T(8,128)(2,1)} %get-tuple-element.229.x_ref, ...), custom_call_target="tpu_custom_call" | custom-call | flops 77309411328 | bytes 60000000 | tf_op jit(solution)/shard_map/bwd/pallas_call | solution.py:467
  838.2 111.4 %bwd.6 = (bf16[4096,768]{1,0:T(8,128)(2,1)}, bf16[4096,768]{1,0:T(8,128)(2,1)}, f32[2048,768]{1,0:T(8,128)}, f32[256,768]{1,0:T(8,128)}, f32[2048,768]{1,0:T(8,128)}) custom-call(s32[16]{0:T(128)} %and_select_fusion.1.wst, s32[160]{0:T(256)} %get-tuple-element.277.dest, s32[1]{0:T(128)} %bitcast.65.total, bf16[4096,768]{1,0:T(8,128)(2,1)} %get-tuple-element.221.x_ref, ...), custom_call_target="tpu_custom_call" | custom-call | flops 77309411328 | bytes 60000000 | tf_op jit(solution)/shard_map/bwd/pallas_call | solution.py:467
  953.2 111.2 %bwd.7 = (bf16[4096,768]{1,0:T(8,128)(2,1)}, bf16[4096,768]{1,0:T(8,128)(2,1)}, f32[2048,768]{1,0:T(8,128)}, f32[256,768]{1,0:T(8,128)}, f32[2048,768]{1,0:T(8,128)}) custom-call(s32[16]{0:T(128)} %and_select_fusion.1.wst, s32[160]{0:T(256)} %get-tuple-element.277.dest, s32[1]{0:T(128)} %bitcast.65.total, bf16[4096,768]{1,0:T(8,128)(2,1)} %get-tuple-element.213.x_ref, ...), custom_call_target="tpu_custom_call" | custom-call | flops 77309411328 | bytes 60000000 | tf_op jit(solution)/shard_map/bwd/pallas_call | solution.py:467
  1071.0 14.6 %shard_map.111 = bf16[4096,768]{1,0:T(8,128)(2,1)} custom-call(s32[4096]{0:T(1024)} %fusion.13.line, bf16[1,4096,768]{2,1,0:T(8,128)(2,1)} %bitcast.233), custom_call_target="tpu_custom_call" | custom-call | flops 10000000000 | bytes 20000000 | tf_op jit(solution)/shard_map/pallas_call | solution.py:527
  1085.6 71.5 %scatter_many.1._ = f32[188640,128]{1,0:T(8,128)} custom-call(s32[4096]{0:T(1024)S(1)} %fusion.15.line, s32[8]{0:T(128)} %get-tuple-element.330.n_base, s32[8]{0:T(128)} %get-tuple-element.329.n_over, s32[8]{0:T(128)} %get-tuple-element.328.at_over, f32[12288,128]{1,0:T(8,128)} %bitcast.84.refs_0_, f32[12288,128]{1,0:T(8,128)} %bitcast.229, ...), custom_call_target="tpu_custom_call" | custom-call | flops 40000000000 | bytes 160000000 | tf_op jit(solution)/shard_map/scatter_many/pallas_call | solution.py:499
  1157.1 9.5 all-to-all-done.14
  1166.6 21.9 %scatter.1 = f32[188640,128]{1,0:T(8,128)} custom-call(s32[4096]{0:T(1024)S(1)} %fusion.15.line, s32[8]{0:T(128)} %get-tuple-element.330.n_base, s32[8]{0:T(128)} %get-tuple-element.329.n_over, s32[8]{0:T(128)} %get-tuple-element.328.at_over, f32[12288,128]{1,0:T(8,128)} %bitcast.78.base_ref, ...), custom_call_target="tpu_custom_call", output_to_operand_aliasing={{}: (6, {})} | custom-call | flops 10000000000 | bytes 40000000 | tf_op jit(solution)/shard_map/scatter/pallas_call | solution.py:484
  (118 shorter events, 83.7 us)
Async XLA Ops:
  47.0 9.0 all-to-all-start.5
  73.8 75.1 %all-to-all-start.6 = ((bf16[8,512,768]{2,1,0:T(8,128)(2,1)}), bf16[8,512,768]{2,1,0:T(8,128)(2,1)}, u32[]{:S(2)}, u32[]{:S(2)}) async-start(bf16[8,512,768]{2,1,0:T(8,128)(2,1)} %bitcast.196), calls=%async_computation.6 | async-start | bytes 12582912 | tf_op jit(solution)/shard_map/all_to_all | solution.py:548
  77.6 24.2 %copy-start = (s32[32,128]{1,0:T(8,128)}, s32[32,128]{1,0:T(8,128)S(1)}, u32[]{:S(2)}) copy-start(s32[32,128]{1,0:T(8,128)S(1)} %reduce-window.32) | copy-start | bytes 49156
  77.8 75.7 %copy-start.2 = (s32[4096]{0:T(1024)}, s32[4096]{0:T(1024)S(1)}, u32[]{:S(2)}) copy-start(s32[4096]{0:T(1024)S(1)} %select_reduce_fusion) | copy-start | bytes 49156
  78.2 23.6 %copy-start.5 = (s32[16,2,128]{2,1,0:T(2,128)}, s32[16,2,128]{2,1,0:T(2,128)S(1)}, u32[]{:S(2)}) copy-start(s32[16,2,128]{2,1,0:T(2,128)S(1)} %broadcast.445) | copy-start | bytes 49156
  148.9 97.9 %all-to-all-start.7 = ((bf16[8,512,768]{2,1,0:T(8,128)(2,1)}), bf16[8,512,768]{2,1,0:T(8,128)(2,1)}, u32[]{:S(2)}, u32[]{:S(2)}) async-start(bf16[8,512,768]{2,1,0:T(8,128)(2,1)} %bitcast.198), calls=%async_computation.7 | async-start | bytes 12582912 | tf_op jit(solution)/shard_map/all_to_all | solution.py:548
  246.8 93.9 %all-to-all-start.8 = ((bf16[8,512,768]{2,1,0:T(8,128)(2,1)}), bf16[8,512,768]{2,1,0:T(8,128)(2,1)}, u32[]{:S(2)}, u32[]{:S(2)}) async-start(bf16[8,512,768]{2,1,0:T(8,128)(2,1)} %bitcast.195), calls=%async_computation.8 | async-start | bytes 12582912 | tf_op jit(solution)/shard_map/all_to_all | solution.py:548
  340.6 79.5 %all-to-all-start.9 = ((bf16[8,512,768]{2,1,0:T(8,128)(2,1)}), bf16[8,512,768]{2,1,0:T(8,128)(2,1)}, u32[]{:S(2)}, u32[]{:S(2)}) async-start(bf16[8,512,768]{2,1,0:T(8,128)(2,1)} %bitcast.197), calls=%async_computation.9 | async-start | bytes 12582912 | tf_op jit(solution)/shard_map/all_to_all | solution.py:548
  420.1 4.7 copy-start.1
  420.1 4.7 copy-start.3
  420.1 4.7 copy-start.6
  420.1 107.4 %all-to-all-start.10 = ((bf16[8,512,768]{2,1,0:T(8,128)(2,1)}), bf16[8,512,768]{2,1,0:T(8,128)(2,1)}, u32[]{:S(2)}, u32[]{:S(2)}) async-start(bf16[8,512,768]{2,1,0:T(8,128)(2,1)} %bitcast.194), calls=%async_computation.10 | async-start | bytes 12582912 | tf_op jit(solution)/shard_map/all_to_all | solution.py:548
  424.5 295.1 %all-gather.6.cloned.1.call-start = ((), (), s32[]{:S(2)}) async-start(), calls=%async_computation.16 | async-start | bytes 7077888 | tf_op jit(solution)/shard_map/all_gather | solution.py:577
  599.6 120.0 %all-to-all-start.11 = ((f32[8,256,768]{2,1,0:T(8,128)}), f32[8,256,768]{2,1,0:T(8,128)}, u32[]{:S(2)}, u32[]{:S(2)}) async-start(f32[8,256,768]{2,1,0:T(8,128)} %bitcast.203), calls=%async_computation.11 | async-start | bytes 12582912 | tf_op jit(solution)/shard_map/all_to_all | solution.py:548
  608.8 225.8 %all-gather.8.cloned.1.call-start = ((), (), s32[]{:S(2)}) async-start(), calls=%async_computation.17 | async-start | bytes 7077888 | tf_op jit(solution)/shard_map/all_gather | solution.py:577
  719.7 114.9 %all-to-all-start.12 = ((f32[8,256,768]{2,1,0:T(8,128)}), f32[8,256,768]{2,1,0:T(8,128)}, u32[]{:S(2)}, u32[]{:S(2)}) async-start(f32[8,256,768]{2,1,0:T(8,128)} %bitcast.201), calls=%async_computation.12 | async-start | bytes 12582912 | tf_op jit(solution)/shard_map/all_to_all | solution.py:548
  723.2 226.4 %all-gather.10.cloned.1.call-start = ((), (), s32[]{:S(2)}) async-start(), calls=%async_computation.18 | async-start | bytes 7077888 | tf_op jit(solution)/shard_map/all_gather | solution.py:577
  834.6 115.0 %all-to-all-start.13 = ((f32[8,256,768]{2,1,0:T(8,128)}), f32[8,256,768]{2,1,0:T(8,128)}, u32[]{:S(2)}, u32[]{:S(2)}) async-start(f32[8,256,768]{2,1,0:T(8,128)} %bitcast.202), calls=%async_computation.13 | async-start | bytes 12582912 | tf_op jit(solution)/shard_map/all_to_all | solution.py:548
  838.1 247.5 %all-gather.14.cloned.1.call-start = ((), (), s32[]{:S(2)}) async-start(), calls=%async_computation.20 | async-start | bytes 7077888 | tf_op jit(solution)/shard_map/all_gather | solution.py:577
  949.6 116.4 %all-to-all-start.15 = ((f32[8,256,768]{2,1,0:T(8,128)}), f32[8,256,768]{2,1,0:T(8,128)}, u32[]{:S(2)}, u32[]{:S(2)}) async-start(f32[8,256,768]{2,1,0:T(8,128)} %bitcast.200), calls=%async_computation.15 | async-start | bytes 12582912 | tf_op jit(solution)/shard_map/all_to_all | solution.py:548
  953.1 213.4 %all-gather.12.cloned.1.call-start = ((), (), s32[]{:S(2)}) async-start(), calls=%async_computation.19 | async-start | bytes 7077888 | tf_op jit(solution)/shard_map/all_gather | solution.py:577
  953.2 111.2 %copy-start.7 = (s32[1,4,8,128]{3,2,1,0:T(8,128)S(1)}, s32[1,4,8,128]{3,2,1,0:T(8,128)}, u32[]{:S(2)}) copy-start(s32[1,4,8,128]{3,2,1,0:T(8,128)} %get-tuple-element.308) | copy-start | bytes 49156
  1066.0 4.3 copy-start.8
  1066.0 100.5 %all-to-all-start.14 = ((f32[8,256,768]{2,1,0:T(8,128)}), f32[8,256,768]{2,1,0:T(8,128)}, u32[]{:S(2)}, u32[]{:S(2)}) async-start(f32[8,256,768]{2,1,0:T(8,128)} %bitcast.199), calls=%async_computation.14 | async-start | bytes 12582912 | tf_op jit(solution)/shard_map/all_to_all | solution.py:548
  (2 other events, 4.4 us)
Sparse Core Ops, SparseCore 0:
  527.7 42.8 all-gather.5
  719.7 84.1 all-gather.7
  834.7 84.1 all-gather.9
  949.7 84.1 all-gather.13
  1064.5 85.8 all-gather.11
